TPU v7x, 32 devices: a whole 2x2x4 slice. The times are simulated.
32 devices in a mesh: rows: 16 (over z, x, core), feat: 2 (over y).
Axes of the slice: x: 2, y: 2, z: 4, core: 2. Of those that a mesh axis runs over, the one named last changes fastest.
Arguments:
- train_cells: bfloat16 [1024, 1536], P('rows', 'feat'), may hold values from -24 to 24
- test_cells: bfloat16 [512, 1536], P('rows', 'feat'), may hold values from -24 to 24
- feat_weights: bfloat16 [4, 192, 192], replicated
- row_weights: bfloat16 [4, 192, 192], replicated
- mlp_up: bfloat16 [192, 768], replicated, may hold values from -0.4375 to 0.4375
- mlp_down: bfloat16 [768, 192], replicated, may hold values from -0.21875 to 0.21875
Outputs:
- train_out: bfloat16 [1024, 1536], P('rows', 'feat')
- test_out: bfloat16 [512, 1536], P('rows', 'feat')
All inputs are finite; a program needn't handle non-finite values.
Results may differ from a plain program's by a relative error of at most 0.017.
Values may be sent and summed in bfloat16 or wider, within the bound.
A program may use at most 128 MiB of HBM per device.

v0:
```python
import functools

import jax
import jax.numpy as jnp
from jax import lax
from jax.experimental import pallas as pl
from jax.experimental.pallas import tpu as pltpu
from jax.sharding import PartitionSpec as P

HD = 32
EPS = 1e-05
LOG2E = 1.4426950408889634
MESH = pl.DeviceIdType.MESH
BF = jnp.bfloat16
F32 = jnp.float32


def layer_norm(x):
    centred = x - jnp.mean(x, axis=-1, keepdims=True)
    spread = jnp.mean(centred * centred, axis=-1, keepdims=True)
    return centred * lax.rsqrt(spread + EPS)


def dot(a, b):
    return jnp.dot(a, b, preferred_element_type=F32)


def dot_t(a, b):
    return lax.dot_general(a, b, (((1,), (1,)), ((), ())), preferred_element_type=F32)


def pack(x):
    n = x.shape[0]
    low = jnp.concatenate([x[: n // 2, 128:], x[n // 2 :, 128:]], axis=1)
    return jnp.concatenate([x[:, :128], low], axis=0)


def unpack(p):
    n = p.shape[0] * 2 // 3
    low = p[n:]
    high = jnp.concatenate([low[:, :64], low[:, 64:]], axis=0)
    return jnp.concatenate([p[:n], high], axis=1)


def gelu(x):
    return 0.5 * x * (1.0 + lax.erf(x * (0.5**0.5)))


def kernel(
    rows_n,
    feats_n,
    train_hbm,
    test_hbm,
    fw_hbm,
    rw_hbm,
    up_hbm,
    down_hbm,
    back_in,
    fw,
    rw,
    up,
    down,
    train_ref,
    test_ref,
    o_train,
    o_test,
    outbox,
    inbox,
    t_outbox,
    t_inbox,
    ring,
    scores,
    values,
    queries,
    back_out,
    w_sem,
    f_send,
    f_recv,
    q_send,
    q_recv,
    r_send,
    r_recv,
    b_send,
    b_recv,
):
    width = fw.shape[-1]
    quad = t_outbox.shape[0]
    heads = width // HD
    groups_n = rows_n // quad
    half = groups_n // 2
    n_train = train_ref.shape[0]
    n_test = test_ref.shape[0]
    n_half = n_train // 2
    scale = LOG2E * HD ** (-0.5)

    my_row = lax.axis_index("rows")
    my_feat = lax.axis_index("feat")
    member = lax.rem(my_row, quad)
    group = my_row // quad

    def partner(k):
        low, high = lax.rem(member, 2), member // 2
        return (1 - high if k // 2 else high) * 2 + (1 - low if k % 2 else low)

    def mate(k):
        return group * quad + partner(k)

    right = lax.rem(group + 1, groups_n) * quad + member
    left = lax.rem(group + groups_n - 1, groups_n) * quad + member
    other = lax.rem(my_feat + 1, feats_n)

    loads = [
        pltpu.make_async_copy(s, d, w_sem.at[i])
        for i, (s, d) in enumerate(
            [
                (train_hbm, train_ref),
                (fw_hbm, fw),
                (test_hbm, test_ref),
                (rw_hbm, rw),
                (up_hbm, up),
                (down_hbm, down),
            ]
        )
    ]
    for c in loads:
        c.start()

    barrier = pltpu.get_barrier_semaphore()
    pl.semaphore_signal(barrier, inc=1, device_id={"feat": other}, device_id_type=MESH)
    for k in range(1, quad):
        pl.semaphore_signal(barrier, inc=1, device_id={"rows": mate(k)}, device_id_type=MESH)
    for d in (right, left):
        pl.semaphore_signal(barrier, inc=1, device_id={"rows": d}, device_id_type=MESH)
    pl.semaphore_wait(barrier, quad + 2)

    halves = [pl.ds(p * n_half, n_half) for p in range(2)]
    swaps = [
        pltpu.make_async_remote_copy(
            src_ref=s,
            dst_ref=d,
            send_sem=f_send.at[i],
            recv_sem=f_recv.at[i],
            device_id={"feat": other},
            device_id_type=MESH,
        )
        for i, (s, d) in enumerate(
            [(train_hbm.at[r], o_train.at[r]) for r in halves] + [(test_hbm, o_test)]
        )
    ]
    for c in swaps:
        c.start()

    def feature_rows(table):
        return jnp.concatenate(
            [table[:, f * width : (f + 1) * width].astype(F32) for f in range(quad)], axis=0
        )

    def split(x):
        n = x.shape[0] // quad
        return [x[f * n : (f + 1) * n] for f in range(quad)]

    def key_value(normed):
        return split(dot(normed, fw[1]).astype(BF)), split(dot(normed, fw[2]).astype(BF))

    same = (
        lax.broadcasted_iota(jnp.int32, (width, width), 0) // HD
        == lax.broadcasted_iota(jnp.int32, (width, width), 1) // HD
    )
    spread = jnp.where(same, 1.0, 0.0).astype(BF)

    def own_side(table):
        cells = feature_rows(table)
        normed = layer_norm(cells).astype(BF)
        q = split((dot(normed, fw[0]) * scale).astype(BF))
        ks, vs = key_value(normed)
        return cells, q, ks, vs

    def feature_attention(own, table):
        cells, q, ks, vs = own
        n = table.shape[0]
        more_k, more_v = key_value(layer_norm(feature_rows(table)).astype(BF))
        ks, vs = ks + more_k, vs + more_v
        mixes = []
        for f in range(quad):
            prod = jnp.concatenate([q[f] * k for k in ks], axis=0)
            s = dot(prod, spread)
            s = [s[g * n : (g + 1) * n] for g in range(len(ks))]
            top = functools.reduce(jnp.maximum, s)
            total = None
            mix = None
            for g in range(len(ks)):
                e = jnp.exp2(s[g] - top)
                t = e * vs[g].astype(F32)
                total = e if total is None else total + e
                mix = t if mix is None else mix + t
            mixes.append((mix / total).astype(BF))
        feat_out = dot(jnp.concatenate(mixes, axis=0), fw[3])
        return split((cells + feat_out).astype(BF))

    def to_mates(box, landing, stage):
        copies = {}
        for k in (2, 3, 1):
            copies[k] = pltpu.make_async_remote_copy(
                src_ref=box.at[partner(k)],
                dst_ref=landing.at[k],
                send_sem=q_send.at[stage, k],
                recv_sem=q_recv.at[stage, k],
                device_id={"rows": mate(k)},
                device_id_type=MESH,
            )
            copies[k].start()
        landing[0] = box[member]
        return copies

    loads[0].wait()
    loads[1].wait()
    own = [own_side(train_ref[p * n_half : (p + 1) * n_half]) for p in range(2)]
    moved = []
    boxes = [(outbox.at[p], inbox.at[p]) for p in range(2)] + [(t_outbox, t_inbox)]
    for p in range(2):
        swaps[p].wait()
        for f, x in enumerate(feature_attention(own[p], o_train[p * n_half : (p + 1) * n_half])):
            outbox[p, f] = pack(x)
        moved.append(to_mates(*boxes[p], p))
    loads[2].wait()
    own_test = own_side(test_ref[...])
    swaps[2].wait()
    for f, x in enumerate(feature_attention(own_test, o_test[...])):
        t_outbox[f] = pack(x)
    moved.append(to_mates(*boxes[2], 2))

    def hop(way, h, p):
        last = h == half - 1
        src = 0 if h == 0 else 2 * h - 1 + way
        dst = 2 * half - 1 if last else 1 + 2 * h + way
        return pltpu.make_async_remote_copy(
            src_ref=ring.at[src, p],
            dst_ref=ring.at[dst, p],
            send_sem=r_send.at[way, h, p],
            recv_sem=r_recv.at[way, h, p],
            device_id={"rows": left if way else right},
            device_id_type=MESH,
        )

    def pieces(way, h):
        return (way,) if h == half - 1 else (way, 1 - way)

    hops = {}
    after = []
    normed = []

    def arrive(stage):
        for k in range(1, quad):
            moved[stage][k].wait_recv()
        landing = boxes[stage][1]
        after.append(
            jnp.concatenate([unpack(landing[k]) for k in range(quad)], axis=0).astype(F32)
        )
        normed.append(layer_norm(after[stage]).astype(BF))

    for p in range(2):
        arrive(p)
        ring[0, p] = pack(normed[p])
        for way in (p, 1 - p):
            if p in pieces(way, 0):
                hops[way, 0, p] = hop(way, 0, p)
                hops[way, 0, p].start()

    loads[3].wait()
    lane_head = lax.broadcasted_iota(jnp.int32, (1, width), 1) // HD
    n_query = quad * (n_train + n_test)
    n_side = n_query // 2
    sizes = [2 * n_half, 2 * n_half, 2 * n_test]
    begins = [0, 2 * n_half, 4 * n_half]
    all_rows = [slice(0, n_query)]
    train_rows = [slice(i * n_side, i * n_side + begins[2]) for i in range(2)]
    test_rows = [slice(i * n_side + begins[2], (i + 1) * n_side) for i in range(2)]
    span = quad * n_train
    values[:, width:] = jnp.ones_like(values[:, width:])

    def ask(stage):
        q_all = (dot(normed[stage], rw[0]) * scale).astype(BF)
        n = sizes[stage]
        for h in range(heads):
            one = jnp.where(lane_head == h, q_all, jnp.zeros_like(q_all))
            for i in range(2):
                at = i * n_side + begins[stage]
                queries[h, at : at + n] = one[(1 - i) * n : (2 - i) * n]

    def take(slot, column):
        x = jnp.concatenate([unpack(ring[slot, 0]), unpack(ring[slot, 1])], axis=0)
        values[column * span : (column + 1) * span, :width] = dot(x, rw[2]).astype(BF)
        return dot(x, rw[1]).astype(BF)

    def score(key, column, rows):
        for h in range(heads):
            for r in rows:
                scores[h, r, column * span : (column + 1) * span] = dot_t(queries[h, r], key)

    def attend(h, rows, columns, carried):
        s = scores[h, rows, columns]
        top = jnp.max(s, axis=-1, keepdims=True)
        if carried is not None:
            top = jnp.maximum(top, carried[0])
        e = jnp.exp2(s - top).astype(BF)
        out = dot(e, values[columns])
        if carried is not None:
            out = out + carried[1] * jnp.exp2(carried[0] - top)
        return top, out

    ask(0)
    ask(1)
    everything = slice(0, n_query)
    if half <= 2:
        own_key = take(0, 0)
        score(own_key, 0, train_rows)
    arrive(2)
    ask(2)
    if half <= 2:
        score(own_key, 0, test_rows)
        states = [attend(h, everything, slice(0, span), None) for h in range(heads)]

    for h in range(half - 1):
        for way in range(2):
            for p in pieces(way, h + 1):
                hops[way, h, p].wait_recv()
                hops[way, h + 1, p] = hop(way, h + 1, p)
                hops[way, h + 1, p].start()
        for way in range(2):
            for p in pieces(way, h):
                if p not in pieces(way, h + 1):
                    hops[way, h, p].wait_recv()

    if half == 2:
        for slot in (1, 2):
            score(take(slot, slot), slot, all_rows)
        states = [
            attend(h, everything, slice(span, 3 * span), states[h]) for h in range(heads)
        ]

    for way in range(2):
        for p in pieces(way, half - 1):
            hops[way, half - 1, p].wait_recv()

    if half <= 2:
        last = 2 * half - 1
        last_key = take(last, last)
        columns = slice(last * span, (last + 1) * span)
    else:
        per = scores.shape[2] // span

        def step(i, states):
            for j in range(per):
                score(take(i * per + j, j), j, all_rows)
            return [attend(h, everything, slice(0, per * span), states[h]) for h in range(heads)]

        start = [
            (
                jnp.full((n_query, 1), -1e30, F32),
                jnp.zeros((n_query, values.shape[1]), F32),
            )
            for _ in range(heads)
        ]
        states = lax.fori_loop(0, groups_n // per, step, start)

    for c in loads[4:]:
        c.wait()
    returns = []
    for i, pair in enumerate(((2, 3), (0, 1))):
        rows = slice(i * n_side, (i + 1) * n_side)
        side = [tuple(x[rows] for x in states[h]) for h in range(heads)]
        if half <= 2:
            score(last_key, last, [rows])
            side = [attend(h, rows, columns, side[h]) for h in range(heads)]
        mixed = None
        for h in range(heads):
            out = side[h][1]
            part = out[:, :width] * (1.0 / out[:, width : width + 1])
            mixed = part if h == 0 else jnp.where(lane_head == h, part, mixed)
        before = [x[(1 - i) * n : (2 - i) * n] for x, n in zip(after, sizes)]
        after_row = jnp.concatenate(before, axis=0) + dot(mixed.astype(BF), rw[3])
        hidden = gelu(dot(layer_norm(after_row).astype(BF), up[...])).astype(BF)
        done = (after_row + dot_t(hidden, down[...])).astype(BF)
        for j, k in enumerate(pair):
            block = pack(
                jnp.concatenate(
                    [
                        done[b + j * (n // 2) : b + (j + 1) * (n // 2)]
                        for b, n in zip(begins, sizes)
                    ],
                    axis=0,
                )
            )
            back_out[k] = block
            if k == 0:
                c = pltpu.make_async_copy(back_out.at[0], back_in.at[member], b_send.at[0])
                c.start()
                returns.append(c)
                continue
            c = pltpu.make_async_remote_copy(
                src_ref=back_out.at[k],
                dst_ref=back_in.at[member],
                send_sem=b_send.at[k],
                recv_sem=b_recv.at[k],
                device_id={"rows": mate(k)},
                device_id_type=MESH,
            )
            c.start()
            returns.append(c)
    for c in returns:
        c.wait()
    for c in [*hops.values(), *(c for m in moved for c in m.values())]:
        c.wait_send()


def place(back_ref, train_out, test_out):
    quad = back_ref.shape[0]
    result = jnp.concatenate([unpack(back_ref[f]) for f in range(quad)], axis=1)
    n_train = train_out.shape[0]
    train_out[...] = result[:n_train]
    test_out[...] = result[n_train:]


def solution(mesh):
    rows_n = mesh.shape["rows"]
    feats_n = mesh.shape["feat"]

    def body(train, test, fw, rw, up, down):
        width = fw.shape[-1]
        quad = train.shape[1] // width
        heads = width // HD
        n_train, n_test = train.shape[0], test.shape[0]
        cell_rows = n_train + n_test
        groups_n = rows_n // quad
        half = groups_n // 2
        span = quad * n_train
        keys = min(groups_n, 4) * span
        packed = cell_rows * width // 128
        vmem = pltpu.VMEM
        dma = pltpu.SemaphoreType.DMA
        vspec = pl.BlockSpec(memory_space=pltpu.VMEM)
        aspec = pl.BlockSpec(memory_space=pl.ANY)
        back = pl.pallas_call(
            functools.partial(kernel, rows_n, feats_n),
            out_shape=pltpu.VMEM((quad, packed, 128), BF),
            in_specs=[aspec, aspec, aspec, aspec, aspec, aspec],
            out_specs=vspec,
            scratch_shapes=[
                vmem(fw.shape, BF),
                vmem(rw.shape, BF),
                vmem(up.shape, BF),
                vmem(down.shape[::-1], BF),
                vmem(train.shape, BF),
                vmem(test.shape, BF),
                vmem(train.shape, BF),
                vmem(test.shape, BF),
                vmem((2, quad, n_train * width // 256, 128), BF),
                vmem((2, quad, n_train * width // 256, 128), BF),
                vmem((quad, n_test * width // 128, 128), BF),
                vmem((quad, n_test * width // 128, 128), BF),
                vmem((groups_n, 2, span * width // 256, 128), BF),
                vmem((heads, quad * cell_rows, keys), F32),
                vmem((keys, 256), BF),
                vmem((heads, quad * cell_rows, width), BF),
                vmem((quad, packed, 128), BF),
                dma((6,)),
                dma((3,)),
                dma((3,)),
                dma((3, quad)),
                dma((3, quad)),
                dma((2, half, 2)),
                dma((2, half, 2)),
                dma((quad,)),
                dma((quad,)),
            ],
            compiler_params=pltpu.CompilerParams(
                collective_id=0, has_side_effects=True, vmem_limit_bytes=60 * 1024 * 1024
            ),
            name="layer",
        )(train, test, fw, rw, up, down.T)
        return pl.pallas_call(
            place,
            out_shape=(
                jax.ShapeDtypeStruct(train.shape, BF),
                jax.ShapeDtypeStruct(test.shape, BF),
            ),
            in_specs=[vspec],
            out_specs=(vspec, vspec),
            name="place",
        )(pltpu.with_memory_space_constraint(back, pltpu.VMEM))

    return jax.shard_map(
        body,
        mesh=mesh,
        in_specs=(P("rows", "feat"), P("rows", "feat"), P(), P(), P(), P()),
        out_specs=(P("rows", "feat"), P("rows", "feat")),
        check_vma=False,
    )
```

profile of v0, /device:TPU:0, one launch (start us, length us, event | category | flops | bytes accessed | tf_op | source)
XLA Modules:
  0.0 29.6 jit_solution(1523394197934754781)
XLA Ops:
  0.6 28.2 %layer.1.back_ref = bf16[4,144,128]{2,1,0:T(8,128)(2,1)S(1)} custom-call(bf16[64,768]{1,0:T(8,128)(2,1)} %train_hbm.1, bf16[32,768]{1,0:T(8,128)(2,1)} %test_hbm.1, bf16[4,192,192]{2,1,0:T(8,128)(2,1)} %fw_hbm.1, bf16[4,192,192]{2,1,0:T(8,128)(2,1)} %rw_hbm.1, bf16[192,768]{1,0:T(8,128)(2,1)} %up_hbm.1, bf16[192,768]{1,0:T(8,128)(2,1)} %bitcast.1), custom_call_target="tpu_custom_call" | custom-call | tf_op jit(solution)/shard_map/layer/pallas_call | solution.py:443
  28.8 0.8 %place.1 = (bf16[64,768]{1,0:T(8,128)(2,1)}, bf16[32,768]{1,0:T(8,128)(2,1)}) custom-call(bf16[4,144,128]{2,1,0:T(8,128)(2,1)S(1)} %layer.1.back_ref), custom_call_target="tpu_custom_call" | custom-call | tf_op jit(solution)/shard_map/place/pallas_call | solution.py:481
where the time goes:
time: 29.8 us; the launch traced here: 29.6 us
  Pallas kernels  29 us (97%)
  between operations  0.64 us (2%)
    pallas_call x1, Pallas kernels, body(): pl.pallas_call(functools.partial(kernel, rows_n, feats_n), out_shape=pltp...  28.2 us
    pallas_call x1, Pallas kernels, body(): pl.pallas_call(place, out_shape=(jax.ShapeDtypeStruct(train.shape, BF), j...  0.79 us

commit v1 on v0

--- a/solution.py
+++ b/solution.py
@@ -413,6 +413,400 @@
         c.wait_send()
 
 
+def unpack_blocks(p):
+    n = p.shape[1] * 2 // 3
+    count = p.shape[0]
+    low = p[:, n:]
+    high = jnp.concatenate([low[:, :, :64], low[:, :, 64:]], axis=1)
+    first = p[:, :n].reshape(count * n, 128)
+    return jnp.concatenate([first, high.reshape(count * n, 64)], axis=1)
+
+
+def plane_kernel(
+    rows_n,
+    feats_n,
+    train_hbm,
+    test_hbm,
+    fw_hbm,
+    rw_hbm,
+    up_hbm,
+    down_hbm,
+    back_in,
+    fw,
+    rw,
+    up,
+    down,
+    train_ref,
+    test_ref,
+    o_train,
+    o_test,
+    zbox,
+    abox,
+    a_in,
+    t_box,
+    t_in,
+    ring,
+    scores,
+    values,
+    queries,
+    back_out,
+    w_sem,
+    f_send,
+    f_recv,
+    a_send,
+    a_recv,
+    r_send,
+    r_recv,
+    b_send,
+    b_recv,
+    gate,
+):
+    width = fw.shape[-1]
+    quad = t_box.shape[0]
+    heads = width // HD
+    groups_n = rows_n // quad
+    n_train = train_ref.shape[0]
+    n_test = test_ref.shape[0]
+    n_half = n_train // 2
+    scale = LOG2E * HD ** (-0.5)
+
+    my_row = lax.axis_index("rows")
+    my_feat = lax.axis_index("feat")
+    member = lax.rem(my_row, quad)
+    group = my_row // quad
+
+    def partner(k):
+        low, high = lax.rem(member, 2), member // 2
+        return (1 - high if k // 2 else high) * 2 + (1 - low if k % 2 else low)
+
+    def mate(k):
+        return group * quad + partner(k)
+
+    right_group = lax.rem(group + 1, groups_n)
+    left_group = lax.rem(group + groups_n - 1, groups_n)
+    right = right_group * quad + member
+    left = left_group * quad + member
+    other = lax.rem(my_feat + 1, feats_n)
+
+    loads = [
+        pltpu.make_async_copy(s, d, w_sem.at[i])
+        for i, (s, d) in enumerate(
+            [
+                (train_hbm, train_ref),
+                (fw_hbm, fw),
+                (test_hbm, test_ref),
+                (rw_hbm, rw),
+                (up_hbm, up),
+                (down_hbm, down),
+            ]
+        )
+    ]
+    for c in loads:
+        c.start()
+
+    barrier = pltpu.get_barrier_semaphore()
+    even = lax.rem(member, 2) == 0
+
+    def greet(**where):
+        pl.semaphore_signal(barrier, inc=1, device_id=where, device_id_type=MESH)
+
+    def tell(i):
+        pl.semaphore_signal(
+            gate.at[i], inc=1, device_id={"rows": mate(1)}, device_id_type=MESH
+        )
+
+    @pl.when(even)
+    def _():
+        greet(rows=my_row, feat=other)
+        for g in (group, right_group, left_group):
+            for m in range(1, quad, 2):
+                greet(rows=g * quad + m)
+        pl.semaphore_wait(barrier, 3)
+        tell(0)
+
+    @pl.when(jnp.logical_not(even))
+    def _():
+        greet(rows=mate(1))
+        greet(rows=mate(1), feat=other)
+        greet(rows=mate(2))
+        for g in (right_group, left_group):
+            for m in range(1, quad, 2):
+                greet(rows=g * quad + m)
+        pl.semaphore_wait(gate.at[0], 1)
+
+    swaps = [
+        pltpu.make_async_remote_copy(
+            src_ref=s,
+            dst_ref=d,
+            send_sem=f_send.at[i],
+            recv_sem=f_recv.at[i],
+            device_id={"feat": other},
+            device_id_type=MESH,
+        )
+        for i, (s, d) in enumerate([(train_hbm, o_train), (test_hbm, o_test)])
+    ]
+    for c in swaps:
+        c.start()
+
+    def feature_rows(table):
+        return jnp.concatenate(
+            [table[:, f * width : (f + 1) * width].astype(F32) for f in range(quad)], axis=0
+        )
+
+    def split(x):
+        n = x.shape[0] // quad
+        return [x[f * n : (f + 1) * n] for f in range(quad)]
+
+    lane_head = lax.broadcasted_iota(jnp.int32, (1, width), 1) // HD
+
+    def by_head(q):
+        return [jnp.where(lane_head == h, q, jnp.zeros_like(q)) for h in range(heads)]
+
+    def join_heads(outs):
+        mixed = None
+        for h, out in enumerate(outs):
+            part = out[:, :width] * (1.0 / out[:, width : width + 1])
+            mixed = part if h == 0 else jnp.where(lane_head == h, part, mixed)
+        return mixed.astype(BF)
+
+    def own_side(table):
+        cells = feature_rows(table)
+        normed = layer_norm(cells).astype(BF)
+        q = (dot(normed, fw[0]) * scale).astype(BF)
+        return cells, q, dot(normed, fw[1]).astype(BF), dot(normed, fw[2]).astype(BF)
+
+    tile = 16
+    n_cells = 2 * quad * tile
+    same_row = (
+        lax.broadcasted_iota(jnp.int32, (heads * quad * tile, n_cells), 0) % tile
+        == lax.broadcasted_iota(jnp.int32, (heads * quad * tile, n_cells), 1) % tile
+    )
+    ones = jnp.ones((n_cells, 256 - width), BF)
+
+    def feature_attention(own, table):
+        cells, q, k, v = own
+        n = table.shape[0]
+        normed = layer_norm(feature_rows(table)).astype(BF)
+        more_k, more_v = dot(normed, fw[1]).astype(BF), dot(normed, fw[2]).astype(BF)
+        mixes = []
+        for b in range(n // tile):
+
+            def rows(x):
+                return [x[f * n + b * tile : f * n + (b + 1) * tile] for f in range(quad)]
+
+            one = jnp.concatenate(by_head(jnp.concatenate(rows(q), axis=0)), axis=0)
+            s = dot_t(one, jnp.concatenate(rows(k) + rows(more_k), axis=0))
+            s = jnp.where(same_row, s, -1e30)
+            e = jnp.exp2(s - jnp.max(s, axis=-1, keepdims=True)).astype(BF)
+            vals = jnp.concatenate(rows(v) + rows(more_v), axis=0)
+            out = dot(e, jnp.concatenate([vals, ones], axis=1))
+            m = quad * tile
+            mixes.append(join_heads([out[h * m : (h + 1) * m] for h in range(heads)]))
+        mix = jnp.concatenate(
+            [x[f * tile : (f + 1) * tile] for f in range(quad) for x in mixes], axis=0
+        )
+        return cells + dot(mix, fw[3])
+
+    def to_mates(box, landing, stage):
+        copies = []
+        for k in (2, 3, 1):
+            copies.append(
+                pltpu.make_async_remote_copy(
+                    src_ref=box.at[partner(k)],
+                    dst_ref=landing.at[k],
+                    send_sem=a_send.at[stage, k],
+                    recv_sem=a_recv.at[stage, k],
+                    device_id={"rows": mate(k)},
+                    device_id_type=MESH,
+                )
+            )
+            copies[-1].start()
+        landing[0] = box[member]
+        return copies
+
+    def to_group(way, p, k):
+        g = left_group if way else right_group
+        return pltpu.make_async_remote_copy(
+            src_ref=zbox.at[p, partner(k)],
+            dst_ref=ring.at[way, p, k],
+            send_sem=r_send.at[way, 0, p],
+            recv_sem=r_recv.at[way, 0, p],
+            device_id={"rows": g * quad + partner(k)},
+            device_id_type=MESH,
+        )
+
+    def whole(way, h, p):
+        return pltpu.make_async_remote_copy(
+            src_ref=ring.at[way, p],
+            dst_ref=ring.at[2 if h else way, p],
+            send_sem=r_send.at[way, h, p],
+            recv_sem=r_recv.at[way, h, p],
+            device_id={"rows": left if way else right},
+            device_id_type=MESH,
+        )
+
+    loads[0].wait()
+    loads[1].wait()
+    own = own_side(train_ref[...])
+
+    @pl.when(jnp.logical_not(even))
+    def _():
+        pl.semaphore_wait(barrier, 3 * quad - 1)
+        tell(1)
+
+    swaps[0].wait()
+    after_own = feature_attention(own, o_train[...])
+    for f, x in enumerate(split(layer_norm(after_own).astype(BF))):
+        for p in range(2):
+            zbox[p, f] = pack(x[p * n_half : (p + 1) * n_half])
+
+    @pl.when(even)
+    def _():
+        pl.semaphore_wait(gate.at[1], 1)
+
+    for way, p in ((0, 0), (1, 1), (0, 1), (1, 0)):
+        for k in range(quad):
+            to_group(way, p, k).start()
+    for f, x in enumerate(split(after_own.astype(BF))):
+        abox[f] = pack(x)
+    moved = [to_mates(abox, a_in, 0)]
+    loads[2].wait()
+    own_test = own_side(test_ref[...])
+    swaps[1].wait()
+    for f, x in enumerate(split(feature_attention(own_test, o_test[...]).astype(BF))):
+        t_box[f] = pack(x)
+    moved.append(to_mates(t_box, t_in, 1))
+
+    after = []
+    normed = []
+
+    def arrive(stage):
+        for c in moved[stage]:
+            c.wait_recv()
+        landing = (a_in, t_in)[stage]
+        after.append(
+            jnp.concatenate([unpack(landing[k]) for k in range(quad)], axis=0).astype(F32)
+        )
+        normed.append(layer_norm(after[stage]).astype(BF))
+
+    n_query = quad * (n_train + n_test)
+    n_side = n_query // 2
+    sizes = [2 * n_train, 2 * n_test]
+    begins = [0, 2 * n_train]
+    train_rows = [slice(i * n_side, i * n_side + begins[1]) for i in range(2)]
+    test_rows = [slice(i * n_side + begins[1], (i + 1) * n_side) for i in range(2)]
+    everything = slice(0, n_query)
+    span = quad * n_train
+
+    def ask(stage):
+        q_all = (dot(normed[stage], rw[0]) * scale).astype(BF)
+        n = sizes[stage]
+        for h, one in enumerate(by_head(q_all)):
+            for i in range(2):
+                at = i * n_side + begins[stage]
+                queries[h, at : at + n] = one[(1 - i) * n : (2 - i) * n]
+
+    def take(x, column):
+        values[column * span : (column + 1) * span, :width] = dot(x, rw[2]).astype(BF)
+        return dot(x, rw[1]).astype(BF)
+
+    def landed(slot):
+        return jnp.concatenate(
+            [unpack_blocks(ring[slot - 1, 0]), unpack_blocks(ring[slot - 1, 1])], axis=0
+        )
+
+    def score(key, column, rows):
+        for h in range(heads):
+            for r in rows:
+                scores[h, r, column * span : (column + 1) * span] = dot_t(queries[h, r], key)
+
+    def attend(h, rows, columns, carried):
+        s = scores[h, rows, columns]
+        top = jnp.max(s, axis=-1, keepdims=True)
+        if carried is not None:
+            top = jnp.maximum(top, carried[0])
+        e = jnp.exp2(s - top).astype(BF)
+        out = dot(e, values[columns])
+        if carried is not None:
+            out = out + carried[1] * jnp.exp2(carried[0] - top)
+        return top, out
+
+    values[:, width:] = jnp.ones_like(values[:, width:])
+    loads[3].wait()
+    arrive(0)
+    ask(0)
+    own_key = take(normed[0], 0)
+    score(own_key, 0, train_rows)
+
+    def relay(way):
+        whole(way, 0, way).wait_recv()
+        whole(way, 1, way).start()
+
+    for way in range(2):
+        relay(way)
+    arrive(1)
+    ask(1)
+    score(own_key, 0, test_rows)
+    states = [attend(h, everything, slice(0, span), None) for h in range(heads)]
+
+    for way in range(2):
+        whole(way, 0, 1 - way).wait_recv()
+    for slot in (1, 2):
+        score(take(landed(slot), slot), slot, [everything])
+    states = [attend(h, everything, slice(span, 3 * span), states[h]) for h in range(heads)]
+
+    for way in range(2):
+        whole(way, 1, way).wait_recv()
+    last_key = take(landed(3), 3)
+    columns = slice(3 * span, 4 * span)
+
+    for c in loads[4:]:
+        c.wait()
+    returns = []
+    for i, pair in enumerate(((2, 3), (0, 1))):
+        rows = slice(i * n_side, (i + 1) * n_side)
+        score(last_key, 3, [rows])
+        side = [
+            attend(h, rows, columns, tuple(x[rows] for x in states[h])) for h in range(heads)
+        ]
+        before = [x[(1 - i) * n : (2 - i) * n] for x, n in zip(after, sizes)]
+        mixed = join_heads([out for _, out in side])
+        after_row = jnp.concatenate(before, axis=0) + dot(mixed, rw[3])
+        hidden = gelu(dot(layer_norm(after_row).astype(BF), up[...])).astype(BF)
+        done = (after_row + dot_t(hidden, down[...])).astype(BF)
+        for j, k in enumerate(pair):
+            back_out[k] = pack(
+                jnp.concatenate(
+                    [
+                        done[b + j * (n // 2) : b + (j + 1) * (n // 2)]
+                        for b, n in zip(begins, sizes)
+                    ],
+                    axis=0,
+                )
+            )
+            if k == 0:
+                c = pltpu.make_async_copy(back_out.at[0], back_in.at[member], b_send.at[0])
+            else:
+                c = pltpu.make_async_remote_copy(
+                    src_ref=back_out.at[k],
+                    dst_ref=back_in.at[member],
+                    send_sem=b_send.at[k],
+                    recv_sem=b_recv.at[k],
+                    device_id={"rows": mate(k)},
+                    device_id_type=MESH,
+                )
+            c.start()
+            returns.append(c)
+    for c in returns:
+        c.wait()
+    for c in [*moved[0], *moved[1]]:
+        c.wait_send()
+    for way in range(2):
+        for p in range(2):
+            whole(way, 0, p).wait_send()
+        whole(way, 1, way).wait_send()
+
+
 def place(back_ref, train_out, test_out):
     quad = back_ref.shape[0]
     result = jnp.concatenate([unpack(back_ref[f]) for f in range(quad)], axis=1)
@@ -440,8 +834,48 @@
         dma = pltpu.SemaphoreType.DMA
         vspec = pl.BlockSpec(memory_space=pltpu.VMEM)
         aspec = pl.BlockSpec(memory_space=pl.ANY)
+        if groups_n == 4 and quad == 4 and n_train % 32 == 0 and n_test % 16 == 0:
+            body_fn = plane_kernel
+            boxes = [
+                vmem((2, quad, n_train * width // 256, 128), BF),
+                vmem((quad, n_train * width // 128, 128), BF),
+                vmem((quad, n_train * width // 128, 128), BF),
+                vmem((quad, n_test * width // 128, 128), BF),
+                vmem((quad, n_test * width // 128, 128), BF),
+                vmem((3, 2, quad, n_train * width // 256, 128), BF),
+            ]
+            flags = [
+                dma((2,)),
+                dma((2,)),
+                dma((2, quad)),
+                dma((2, quad)),
+                dma((2, 2, 2)),
+                dma((2, 2, 2)),
+                dma((quad,)),
+                dma((quad,)),
+                pltpu.SemaphoreType.REGULAR((2,)),
+            ]
+        else:
+            body_fn = kernel
+            boxes = [
+                vmem((2, quad, n_train * width // 256, 128), BF),
+                vmem((2, quad, n_train * width // 256, 128), BF),
+                vmem((quad, n_test * width // 128, 128), BF),
+                vmem((quad, n_test * width // 128, 128), BF),
+                vmem((groups_n, 2, span * width // 256, 128), BF),
+            ]
+            flags = [
+                dma((3,)),
+                dma((3,)),
+                dma((3, quad)),
+                dma((3, quad)),
+                dma((2, half, 2)),
+                dma((2, half, 2)),
+                dma((quad,)),
+                dma((quad,)),
+            ]
         back = pl.pallas_call(
-            functools.partial(kernel, rows_n, feats_n),
+            functools.partial(body_fn, rows_n, feats_n),
             out_shape=pltpu.VMEM((quad, packed, 128), BF),
             in_specs=[aspec, aspec, aspec, aspec, aspec, aspec],
             out_specs=vspec,
@@ -454,24 +888,13 @@
                 vmem(test.shape, BF),
                 vmem(train.shape, BF),
                 vmem(test.shape, BF),
-                vmem((2, quad, n_train * width // 256, 128), BF),
-                vmem((2, quad, n_train * width // 256, 128), BF),
-                vmem((quad, n_test * width // 128, 128), BF),
-                vmem((quad, n_test * width // 128, 128), BF),
-                vmem((groups_n, 2, span * width // 256, 128), BF),
+                *boxes,
                 vmem((heads, quad * cell_rows, keys), F32),
                 vmem((keys, 256), BF),
                 vmem((heads, quad * cell_rows, width), BF),
                 vmem((quad, packed, 128), BF),
                 dma((6,)),
-                dma((3,)),
-                dma((3,)),
-                dma((3, quad)),
-                dma((3, quad)),
-                dma((2, half, 2)),
-                dma((2, half, 2)),
-                dma((quad,)),
-                dma((quad,)),
+                *flags,
             ],
             compiler_params=pltpu.CompilerParams(
                 collective_id=0, has_side_effects=True, vmem_limit_bytes=60 * 1024 * 1024

time: 29.8 us -> 26.9 us (0.903)
  Pallas kernels: 29 us -> 26.1 us
    pallas_call x1, Pallas kernels: 28.2 us -> 25.3 us  [body(): pl.pallas_call(functools.partial(body_fn, rows_n, feats_n), out_shape=plt...]
where the time goes in v1:
time: 26.9 us; the launch traced here: 26.7 us
  Pallas kernels  26.1 us (97%)
  between operations  0.64 us (2%)
    pallas_call x1, Pallas kernels, body(): pl.pallas_call(functools.partial(body_fn, rows_n, feats_n), out_shape=plt...  25.3 us
    pallas_call x1, Pallas kernels, body(): pl.pallas_call(place, out_shape=(jax.ShapeDtypeStruct(train.shape, BF), j...  0.79 us

profile of v1, /device:TPU:0, one launch (start us, length us, event | category | flops | bytes accessed | tf_op | source)
XLA Modules:
  0.0 26.7 jit_solution(12325491992298630932)
XLA Ops:
  0.6 25.3 %layer.1.back_ref = bf16[4,144,128]{2,1,0:T(8,128)(2,1)S(1)} custom-call(bf16[64,768]{1,0:T(8,128)(2,1)} %train_hbm.1, bf16[32,768]{1,0:T(8,128)(2,1)} %test_hbm.1, bf16[4,192,192]{2,1,0:T(8,128)(2,1)} %fw_hbm.1, bf16[4,192,192]{2,1,0:T(8,128)(2,1)} %rw_hbm.1, bf16[192,768]{1,0:T(8,128)(2,1)} %up_hbm.1, bf16[192,768]{1,0:T(8,128)(2,1)} %bitcast.1), custom_call_target="tpu_custom_call" | custom-call | tf_op jit(solution)/shard_map/layer/pallas_call | solution.py:877
  25.9 0.8 %place.1 = (bf16[64,768]{1,0:T(8,128)(2,1)}, bf16[32,768]{1,0:T(8,128)(2,1)}) custom-call(bf16[4,144,128]{2,1,0:T(8,128)(2,1)S(1)} %layer.1.back_ref), custom_call_target="tpu_custom_call" | custom-call | tf_op jit(solution)/shard_map/place/pallas_call | solution.py:904

commit v2 on v0

--- a/solution.py
+++ b/solution.py
@@ -413,6 +413,508 @@
         c.wait_send()
 
 
+def unpack_blocks(p):
+    n = p.shape[1] * 2 // 3
+    count = p.shape[0]
+    low = p[:, n:]
+    high = jnp.concatenate([low[:, :, :64], low[:, :, 64:]], axis=1)
+    first = p[:, :n].reshape(count * n, 128)
+    return jnp.concatenate([first, high.reshape(count * n, 64)], axis=1)
+
+
+def plane_kernel(
+    rows_n,
+    feats_n,
+    train_hbm,
+    test_hbm,
+    fw_hbm,
+    rw_hbm,
+    up_hbm,
+    down_hbm,
+    back_in,
+    fw,
+    rw,
+    up,
+    down,
+    train_ref,
+    test_ref,
+    o_train,
+    o_test,
+    zbox,
+    abox,
+    a_in,
+    t_box,
+    t_in,
+    ring,
+    early_q,
+    late_q,
+    early_x,
+    late_x,
+    fw_t,
+    f_cells,
+    f_x,
+    t_cells,
+    t_x,
+    fq,
+    fk,
+    fv,
+    fs,
+    fe,
+    fm,
+    rw_t,
+    up_t,
+    early_s,
+    late_s,
+    early_e,
+    late_e,
+    early_sum,
+    late_sum,
+    early_top,
+    late_top,
+    keys,
+    vals,
+    raised,
+    hidden,
+    back_out,
+    w_sem,
+    f_send,
+    f_recv,
+    a_send,
+    a_recv,
+    r_send,
+    r_recv,
+    b_send,
+    b_recv,
+    gate,
+):
+    width = fw.shape[-1]
+    quad = t_box.shape[1]
+    heads = width // HD
+    groups_n = rows_n // quad
+    n_train = train_ref.shape[0]
+    n_test = test_ref.shape[0]
+    n_half, n_quart = n_train // 2, n_test // 2
+    scale = LOG2E * HD ** (-0.5)
+
+    my_row = lax.axis_index("rows")
+    my_feat = lax.axis_index("feat")
+    member = lax.rem(my_row, quad)
+    group = my_row // quad
+
+    def partner(k):
+        low, high = lax.rem(member, 2), member // 2
+        return (1 - high if k // 2 else high) * 2 + (1 - low if k % 2 else low)
+
+    def mate(k):
+        return group * quad + partner(k)
+
+    right_group = lax.rem(group + 1, groups_n)
+    left_group = lax.rem(group + groups_n - 1, groups_n)
+    right = right_group * quad + member
+    left = left_group * quad + member
+    other = lax.rem(my_feat + 1, feats_n)
+
+    loads = [
+        pltpu.make_async_copy(s, d, w_sem.at[i])
+        for i, (s, d) in enumerate(
+            [
+                (train_hbm, train_ref),
+                (fw_hbm, fw),
+                (test_hbm, test_ref),
+                (rw_hbm, rw),
+                (up_hbm, up),
+                (down_hbm, down),
+            ]
+        )
+    ]
+    for c in loads:
+        c.start()
+
+    barrier = pltpu.get_barrier_semaphore()
+    even = lax.rem(member, 2) == 0
+
+    def greet(**where):
+        pl.semaphore_signal(barrier, inc=1, device_id=where, device_id_type=MESH)
+
+    def tell(i):
+        pl.semaphore_signal(
+            gate.at[i], inc=1, device_id={"rows": mate(1)}, device_id_type=MESH
+        )
+
+    @pl.when(even)
+    def _():
+        greet(rows=my_row, feat=other)
+        for g in (group, right_group, left_group):
+            for m in range(1, quad, 2):
+                for y in (my_feat, other):
+                    greet(rows=g * quad + m, feat=y)
+        pl.semaphore_wait(barrier, 3)
+        tell(0)
+
+    @pl.when(jnp.logical_not(even))
+    def _():
+        greet(rows=mate(1))
+        greet(rows=mate(1), feat=other)
+        greet(rows=my_row, feat=other)
+        for y in (my_feat, other):
+            greet(rows=mate(2), feat=y)
+            for g in (right_group, left_group):
+                for m in range(1, quad, 2):
+                    greet(rows=g * quad + m, feat=y)
+        pl.semaphore_wait(gate.at[0], 1)
+
+    swaps = [
+        pltpu.make_async_remote_copy(
+            src_ref=s,
+            dst_ref=d,
+            send_sem=f_send.at[i],
+            recv_sem=f_recv.at[i],
+            device_id={"feat": other},
+            device_id_type=MESH,
+        )
+        for i, (s, d) in enumerate(
+            [
+                (train_hbm.at[pl.ds(pl.multiple_of(other * n_half, n_half), n_half)], o_train),
+                (test_hbm.at[pl.ds(pl.multiple_of(other * n_quart, n_quart), n_quart)], o_test),
+            ]
+        )
+    ]
+    for c in swaps:
+        c.start()
+
+    tile = 16
+    cell = quad * tile
+    pair = 2 * cell
+    lines = HD + 16
+    same_row = (
+        lax.broadcasted_iota(jnp.int32, (pair, heads * pair), 0) % tile
+        == lax.broadcasted_iota(jnp.int32, (pair, heads * pair), 1) % tile
+    )
+
+    def fill(table, side, cells_ref, x_ref):
+        n = table.shape[0] // tile
+        cells = jnp.concatenate(
+            [
+                table[b * tile : (b + 1) * tile, f * width : (f + 1) * width].astype(F32)
+                for b in range(n)
+                for f in range(quad)
+            ],
+            axis=0,
+        )
+        normed = layer_norm(cells).astype(BF)
+        for b in range(n):
+            to = slice((2 * b + side) * cell, (2 * b + side + 1) * cell)
+            cells_ref[to] = cells[b * cell : (b + 1) * cell]
+            x_ref[to] = normed[b * cell : (b + 1) * cell]
+
+    def normed_columns(x):
+        centred = x - jnp.mean(x, axis=0, keepdims=True)
+        spread = jnp.mean(centred * centred, axis=0, keepdims=True)
+        return centred * lax.rsqrt(spread + EPS)
+
+    def feature_attention(cells_ref, x_ref):
+        n = x_ref.shape[0]
+        blocks = [slice(b * pair, (b + 1) * pair) for b in range(n // pair)]
+        x = x_ref[...]
+        q = (dot_t(fw_t[0], x) * scale).astype(BF)
+        fk[:n] = dot(x, fw[1]).astype(BF)
+        v = dot_t(fw_t[2], x).astype(BF)
+        for h in range(heads):
+            rows = slice(h * HD, (h + 1) * HD)
+            fv[h * lines : h * lines + HD, :n] = v[rows]
+            for b, at in enumerate(blocks):
+                fq[rows, (b * heads + h) * pair : (b * heads + h + 1) * pair] = q[rows, at]
+        for b, at in enumerate(blocks):
+            fs[at] = dot(fk[at], fq[:, b * heads * pair : (b + 1) * heads * pair])
+        for at in blocks:
+            s = jnp.where(same_row, fs[at], -1e30)
+            fe[at] = jnp.exp2(s - jnp.max(s, axis=0, keepdims=True)).astype(BF)
+        for at in blocks:
+            for h in range(heads):
+                out = dot(
+                    fv[h * lines : (h + 1) * lines, at], fe[at, h * pair : (h + 1) * pair]
+                )
+                part = out[:HD] * (1.0 / out[HD : HD + 1])
+                fm[h * HD : (h + 1) * HD, at] = part.astype(BF)
+        after = cells_ref[...].T + dot(fw_t[3], fm[:, :n])
+        return after, normed_columns(after)
+
+    def sides(x):
+        n = x.shape[0] // pair
+        for j in range(2):
+            for f in range(quad):
+                at = [(2 * b + j) * cell + f * tile for b in range(n)]
+                yield j, f, jnp.concatenate([x[i : i + tile] for i in at], axis=0)
+
+    feats = (my_feat, other)
+
+    def to_mates(box, landing, stage):
+        copies = []
+        for k, j in ((2, 0), (0, 1), (3, 0), (1, 1), (2, 1), (3, 1), (1, 0)):
+            copies.append(
+                pltpu.make_async_remote_copy(
+                    src_ref=box.at[j, partner(k)],
+                    dst_ref=landing.at[j, k],
+                    send_sem=a_send.at[stage, j, k],
+                    recv_sem=a_recv.at[stage, j, k],
+                    device_id={"rows": mate(k), "feat": feats[j]},
+                    device_id_type=MESH,
+                )
+            )
+            copies[-1].start()
+        landing[0, 0] = box[0, member]
+        return copies
+
+    inner = jnp.logical_and(group > 0, group < groups_n - 1)
+
+    def to_group(way, p, k):
+        g = jnp.where(way == 1, left_group, right_group)
+        return pltpu.make_async_remote_copy(
+            src_ref=zbox.at[p, partner(k)],
+            dst_ref=ring.at[way, p, k],
+            send_sem=r_send.at[way, p],
+            recv_sem=r_recv.at[way, p],
+            device_id={"rows": g * quad + partner(k), "feat": feats[p]},
+            device_id_type=MESH,
+        )
+
+    def whole(slot, p):
+        return pltpu.make_async_remote_copy(
+            src_ref=ring.at[slot, p],
+            dst_ref=ring.at[slot, p],
+            send_sem=r_send.at[slot, p],
+            recv_sem=r_recv.at[slot, p],
+            device_id={"rows": right},
+            device_id_type=MESH,
+        )
+
+    def onward(way, p):
+        return pltpu.make_async_remote_copy(
+            src_ref=ring.at[way, p],
+            dst_ref=ring.at[2, p],
+            send_sem=r_send.at[2 + way, p],
+            recv_sem=r_recv.at[2, p],
+            device_id={"rows": left if way else right},
+            device_id_type=MESH,
+        )
+
+    def relay(p):
+        @pl.when(inner)
+        def _():
+            for way in range(2):
+                whole(way, p).wait_recv()
+                onward(way, p).start()
+
+    loads[0].wait()
+    loads[1].wait()
+    fill(train_ref[pl.ds(pl.multiple_of(my_feat * n_half, n_half), n_half)], 0, f_cells, f_x)
+    for i in (0, 2, 3):
+        fw_t[i] = fw[i].astype(F32).T.astype(BF)
+    loads[2].wait()
+    fill(test_ref[pl.ds(pl.multiple_of(my_feat * n_quart, n_quart), n_quart)], 0, t_cells, t_x)
+    fq[...] = jnp.zeros_like(fq)
+    fv[...] = jnp.ones_like(fv)
+
+    @pl.when(jnp.logical_not(even))
+    def _():
+        pl.semaphore_wait(barrier, 6 * quad - 1)
+        tell(1)
+
+    swaps[0].wait()
+    fill(o_train[...], 1, f_cells, f_x)
+    after_own, normed_own = feature_attention(f_cells, f_x)
+    for j, f, x in sides(normed_own.T):
+        zbox[j, f] = pack(x.astype(BF))
+
+    @pl.when(even)
+    def _():
+        pl.semaphore_wait(gate.at[1], 1)
+
+    near = jnp.where(group == groups_n - 1, 1, 0)
+    for way in (near, 1 - near):
+        for p in range(2):
+            for k in range(quad):
+                to_group(way, p, k).start()
+    for j, f, x in sides(after_own.T):
+        abox[j, f] = pack(x.astype(BF))
+    moved = [to_mates(abox, a_in, 0)]
+    swaps[1].wait()
+    fill(o_test[...], 1, t_cells, t_x)
+    after_own, _ = feature_attention(t_cells, t_x)
+    for j, f, x in sides(after_own.T):
+        t_box[j, f] = pack(x.astype(BF))
+    moved.append(to_mates(t_box, t_in, 1))
+
+    loads[3].wait()
+    for i in (0, 2, 3):
+        rw_t[i] = rw[i].astype(F32).T.astype(BF)
+    loads[4].wait()
+    up_t[...] = up[...].astype(F32).T.astype(BF)
+    vals[...] = jnp.ones_like(vals)
+    early_q[...] = jnp.zeros_like(early_q)
+    late_q[...] = jnp.zeros_like(late_q)
+
+    def arrive(stage):
+        for c in moved[stage]:
+            c.wait_recv()
+        landing = (a_in, t_in)[stage]
+        x = jnp.concatenate(
+            [unpack(landing[j, k]) for k in range(quad) for j in range(2)], axis=0
+        ).astype(F32)
+        normed = layer_norm(x).astype(BF)
+        return x, normed, (dot_t(rw_t[0], normed) * scale).astype(BF)
+
+    n_mid = 2 * n_train
+    n_late = 2 * n_train
+    n_early = n_mid + quad * n_test
+
+    def place_queries(q, into, size, at):
+        n = q.shape[1]
+        for h in range(heads):
+            rows = slice(h * HD, (h + 1) * HD)
+            into[rows, h * size + at : h * size + at + n] = q[rows]
+
+    late = (late_q, late_s, late_e, late_sum, late_top, n_late)
+    early = (early_q, early_s, early_e, early_sum, early_top, n_early)
+
+    def key_value_rows(x, i):
+        keys[i] = dot(x, rw[1]).astype(BF)
+        value = dot_t(rw_t[2], x).astype(BF)
+        for h in range(heads):
+            vals[i, h * lines : h * lines + HD] = value[h * HD : (h + 1) * HD]
+
+    def attend(asked, i, first=False):
+        per_head = [
+            (part, h, slice(h * part[5], (h + 1) * part[5]), slice(h * lines, (h + 1) * lines))
+            for part in asked
+            for h in range(heads)
+        ]
+        key = keys[i]
+        for (q, s, _, _, _, _), h, c, _ in per_head:
+            s[:, c] = dot(key, q[:, c])
+        for (_, s, e, total, tops, _), h, c, r in per_head:
+            top = jnp.max(s[:, c], axis=0, keepdims=True)
+            if not first:
+                old = tops[0:1, c]
+                top = jnp.maximum(top, old)
+                total[r] = total[r] * jnp.exp2(old - top)
+            e[:, c] = jnp.exp2(s[:, c] - top).astype(BF)
+            tops[0:1, c] = top
+        for (_, _, e, total, _, _), h, c, r in per_head:
+            out = dot(vals[i, r], e[:, c])
+            total[r] = out if first else total[r] + out
+
+    def finish(part, before):
+        total = part[3]
+        mix = jnp.concatenate(
+            [
+                total[h * lines : h * lines + HD]
+                * (1.0 / total[h * lines + HD : h * lines + HD + 1])
+                for h in range(heads)
+            ],
+            axis=0,
+        ).astype(BF)
+        after_row = before + dot(rw_t[3], mix)
+        normed = normed_columns(after_row).astype(BF)
+        n = normed.shape[1]
+        raised[:, :n] = dot(up_t[...], normed)
+        hidden[:, :n] = gelu(raised[:, :n]).astype(BF)
+        return (after_row + dot(down[...], hidden[:, :n])).T.astype(BF)
+
+    relay(0)
+    relay(1)
+    x, normed, q = arrive(0)
+    place_queries(q[:, n_mid:], early_q, n_early, 0)
+    place_queries(q[:, :n_late], late_q, n_late, 0)
+    early_x[:, :n_mid] = x[n_late:].T
+    late_x[...] = x[:n_late].T
+    key_value_rows(normed, 0)
+    attend([late], 0, True)
+    x, _, q = arrive(1)
+    place_queries(q, early_q, n_early, n_mid)
+    early_x[:, n_mid:] = x.T
+    attend([early], 0, True)
+
+    at_start, at_end = group == 0, group == groups_n - 1
+    order = (
+        jnp.where(at_start, 1, 0),
+        jnp.where(at_start, 2, jnp.where(at_end, 2, 1)),
+        jnp.where(at_start, 0, jnp.where(at_end, 1, 2)),
+    )
+
+    def fetch(i):
+        slot = order[i]
+
+        @pl.when(jnp.logical_not(jnp.logical_and(inner, slot < 2)))
+        def _():
+            for p in range(2):
+                whole(slot, p).wait_recv()
+
+        x = jnp.concatenate([unpack_blocks(ring[slot, p]) for p in range(2)], axis=0)
+        key_value_rows(x, (i + 1) % 2)
+
+    for i in range(2):
+        fetch(i)
+        attend([late, early], (i + 1) % 2)
+    fetch(2)
+    loads[5].wait()
+
+    returns = []
+
+    def give_back(k, done, tests):
+        block = jnp.concatenate([done, tests[k * n_test : (k + 1) * n_test]], axis=0)
+        back_out[k] = pack(block)
+        if k == 0:
+            c = pltpu.make_async_copy(back_out.at[0], back_in.at[member], b_send.at[0])
+        else:
+            c = pltpu.make_async_remote_copy(
+                src_ref=back_out.at[k],
+                dst_ref=back_in.at[member],
+                send_sem=b_send.at[k],
+                recv_sem=b_recv.at[k],
+                device_id={"rows": mate(k)},
+                device_id_type=MESH,
+            )
+        c.start()
+        returns.append(c)
+
+    attend([early], 1)
+    done = finish(early, early_x[...])
+    tests = done[n_mid:]
+    for k in (2, 3):
+        give_back(k, done[(k - 2) * n_train : (k - 1) * n_train], tests)
+    attend([late], 1)
+    done = finish(late, late_x[...])
+    for k in (1, 0):
+        give_back(k, done[k * n_train : (k + 1) * n_train], tests)
+    for c in returns:
+        c.wait()
+    for c in [*moved[0], *moved[1]]:
+        c.wait_send()
+    for way in range(2):
+        for p in range(2):
+            whole(way, p).wait_send()
+
+    @pl.when(inner)
+    def _():
+        for way in range(2):
+            for p in range(2):
+                onward(way, p).wait_send()
+
+
+def place_halves(back_ref, train_out, test_out):
+    quad = back_ref.shape[0]
+    result = jnp.concatenate([unpack(back_ref[f]) for f in range(quad)], axis=1)
+    in_order = lax.axis_index("feat") == 0
+    begin = 0
+    for out in (train_out, test_out):
+        half = out.shape[0] // 2
+        one, two = (result[begin + j * half : begin + (j + 1) * half] for j in range(2))
+        out[:half] = jnp.where(in_order, one, two)
+        out[half:] = jnp.where(in_order, two, one)
+        begin += 2 * half
+
+
 def place(back_ref, train_out, test_out):
     quad = back_ref.shape[0]
     result = jnp.concatenate([unpack(back_ref[f]) for f in range(quad)], axis=1)
@@ -440,30 +942,83 @@
         dma = pltpu.SemaphoreType.DMA
         vspec = pl.BlockSpec(memory_space=pltpu.VMEM)
         aspec = pl.BlockSpec(memory_space=pl.ANY)
-        back = pl.pallas_call(
-            functools.partial(kernel, rows_n, feats_n),
-            out_shape=pltpu.VMEM((quad, packed, 128), BF),
-            in_specs=[aspec, aspec, aspec, aspec, aspec, aspec],
-            out_specs=vspec,
-            scratch_shapes=[
+        weights = (fw, rw, up, down.T)
+        place_fn = place
+        fits = groups_n == 4 and quad == 4 and feats_n == 2
+        if fits and n_train % 32 == 0 and n_test % 32 == 0:
+            body_fn, place_fn = plane_kernel, place_halves
+            n_half, n_quart = n_train // 2, n_test // 2
+            swapped = [vmem((n_half, quad * width), BF), vmem((n_quart, quad * width), BF)]
+            both = 2 * quad
+            pair = both * 16
+            lines = heads * (HD + 16)
+            early, late = 2 * n_train + quad * n_test, 2 * n_train
+            work = [
+                vmem((width, heads * early), BF),
+                vmem((width, heads * late), BF),
+                vmem((width, early), F32),
+                vmem((width, late), F32),
                 vmem(fw.shape, BF),
+                vmem((both * n_half, width), F32),
+                vmem((both * n_half, width), BF),
+                vmem((both * n_quart, width), F32),
+                vmem((both * n_quart, width), BF),
+                vmem((width, heads * both * n_half), BF),
+                vmem((both * n_half, width), BF),
+                vmem((lines, both * n_half), BF),
+                vmem((both * n_half, heads * pair), F32),
+                vmem((both * n_half, heads * pair), BF),
+                vmem((width, both * n_half), BF),
                 vmem(rw.shape, BF),
-                vmem(up.shape, BF),
-                vmem(down.shape[::-1], BF),
-                vmem(train.shape, BF),
-                vmem(test.shape, BF),
-                vmem(train.shape, BF),
-                vmem(test.shape, BF),
+                vmem(up.shape[::-1], BF),
+                vmem((span, heads * early), F32),
+                vmem((span, heads * late), F32),
+                vmem((span, heads * early), BF),
+                vmem((span, heads * late), BF),
+                vmem((heads * (HD + 16), early), F32),
+                vmem((heads * (HD + 16), late), F32),
+                vmem((8, heads * early), F32),
+                vmem((8, heads * late), F32),
+                vmem((2, span, width), BF),
+                vmem((2, heads * (HD + 16), span), BF),
+                vmem((up.shape[1], early), F32),
+                vmem((up.shape[1], early), BF),
+            ]
+            boxes = [
+                vmem((2, quad, n_train * width // 256, 128), BF),
+                vmem((2, quad, n_train * width // 256, 128), BF),
+                vmem((2, quad, n_train * width // 256, 128), BF),
+                vmem((2, quad, n_test * width // 256, 128), BF),
+                vmem((2, quad, n_test * width // 256, 128), BF),
+                vmem((3, 2, quad, n_train * width // 256, 128), BF),
+            ]
+            flags = [
+                dma((2,)),
+                dma((2,)),
+                dma((2, 2, quad)),
+                dma((2, 2, quad)),
+                dma((4, 2)),
+                dma((3, 2)),
+                dma((quad,)),
+                dma((quad,)),
+                pltpu.SemaphoreType.REGULAR((2,)),
+            ]
+        else:
+            body_fn = kernel
+            swapped = [vmem(train.shape, BF), vmem(test.shape, BF)]
+            work = [
+                vmem((heads, quad * cell_rows, keys), F32),
+                vmem((keys, 256), BF),
+                vmem((heads, quad * cell_rows, width), BF),
+            ]
+            boxes = [
                 vmem((2, quad, n_train * width // 256, 128), BF),
                 vmem((2, quad, n_train * width // 256, 128), BF),
                 vmem((quad, n_test * width // 128, 128), BF),
                 vmem((quad, n_test * width // 128, 128), BF),
                 vmem((groups_n, 2, span * width // 256, 128), BF),
-                vmem((heads, quad * cell_rows, keys), F32),
-                vmem((keys, 256), BF),
-                vmem((heads, quad * cell_rows, width), BF),
-                vmem((quad, packed, 128), BF),
-                dma((6,)),
+            ]
+            flags = [
                 dma((3,)),
                 dma((3,)),
                 dma((3, quad)),
@@ -472,14 +1027,30 @@
                 dma((2, half, 2)),
                 dma((quad,)),
                 dma((quad,)),
+            ]
+        back = pl.pallas_call(
+            functools.partial(body_fn, rows_n, feats_n),
+            out_shape=pltpu.VMEM((quad, packed, 128), BF),
+            in_specs=[aspec, aspec, aspec, aspec, aspec, aspec],
+            out_specs=vspec,
+            scratch_shapes=[
+                *(vmem(w.shape, BF) for w in weights),
+                vmem(train.shape, BF),
+                vmem(test.shape, BF),
+                *swapped,
+                *boxes,
+                *work,
+                vmem((quad, packed, 128), BF),
+                dma((6,)),
+                *flags,
             ],
             compiler_params=pltpu.CompilerParams(
                 collective_id=0, has_side_effects=True, vmem_limit_bytes=60 * 1024 * 1024
             ),
             name="layer",
-        )(train, test, fw, rw, up, down.T)
+        )(train, test, *weights)
         return pl.pallas_call(
-            place,
+            place_fn,
             out_shape=(
                 jax.ShapeDtypeStruct(train.shape, BF),
                 jax.ShapeDtypeStruct(test.shape, BF),

time: 29.8 us -> 26.4 us (0.89)
  Pallas kernels: 29 us -> 25.6 us
    pallas_call x2, Pallas kernels: 29 us -> 25.6 us  [the longest x1 24.8 us: body(): pl.pallas_call(functools.partial(body_fn, rows_n, feats_n), out_shape=plt...]
where the time goes in v2:
time: 26.4 us; the launch traced here: 26.2 us
  Pallas kernels  25.6 us (97%)
  between operations  0.64 us (2%)
    pallas_call x1, Pallas kernels, body(): pl.pallas_call(functools.partial(body_fn, rows_n, feats_n), out_shape=plt...  24.8 us
    pallas_call x1, Pallas kernels, body(): pl.pallas_call(place_fn, out_shape=(jax.ShapeDtypeStruct(train.shape, BF)...  0.79 us

profile of v2, /device:TPU:0, one launch (start us, length us, event | category | flops | bytes accessed | tf_op | source)
XLA Modules:
  0.0 26.2 jit_solution(6320267621941628886)
XLA Ops:
  0.6 24.8 %layer.1.back_ref = bf16[4,144,128]{2,1,0:T(8,128)(2,1)S(1)} custom-call(bf16[64,768]{1,0:T(8,128)(2,1)} %train_hbm.1, bf16[32,768]{1,0:T(8,128)(2,1)} %test_hbm.1, bf16[4,192,192]{2,1,0:T(8,128)(2,1)} %fw_hbm.1, bf16[4,192,192]{2,1,0:T(8,128)(2,1)} %rw_hbm.1, bf16[192,768]{1,0:T(8,128)(2,1)} %up_hbm.1, bf16[192,768]{1,0:T(8,128)(2,1)} %bitcast.1), custom_call_target="tpu_custom_call" | custom-call | tf_op jit(solution)/shard_map/layer/pallas_call | solution.py:1031
  25.5 0.8 %place.1 = (bf16[64,768]{1,0:T(8,128)(2,1)}, bf16[32,768]{1,0:T(8,128)(2,1)}) custom-call(bf16[4,144,128]{2,1,0:T(8,128)(2,1)S(1)} %layer.1.back_ref), custom_call_target="tpu_custom_call" | custom-call | tf_op jit(solution)/shard_map/place/pallas_call | solution.py:1052

commit v3 on v2

--- a/solution.py
+++ b/solution.py
@@ -462,6 +462,7 @@
     fe,
     fm,
     rw_t,
+    asks,
     up_t,
     early_s,
     late_s,
@@ -651,19 +652,26 @@
     def to_mates(box, landing, stage):
         copies = []
         for k, j in ((2, 0), (0, 1), (3, 0), (1, 1), (2, 1), (3, 1), (1, 0)):
-            copies.append(
-                pltpu.make_async_remote_copy(
-                    src_ref=box.at[j, partner(k)],
-                    dst_ref=landing.at[j, k],
-                    send_sem=a_send.at[stage, j, k],
-                    recv_sem=a_recv.at[stage, j, k],
-                    device_id={"rows": mate(k), "feat": feats[j]},
-                    device_id_type=MESH,
-                )
+            pltpu.make_async_remote_copy(
+                src_ref=box.at[j, partner(k)],
+                dst_ref=landing.at[j, k],
+                send_sem=a_send.at[stage, j],
+                recv_sem=a_recv.at[stage, j],
+                device_id={"rows": mate(k), "feat": feats[j]},
+                device_id_type=MESH,
+            ).start()
+        landing[0, 0] = box[0, member]
+        return [
+            pltpu.make_async_remote_copy(
+                src_ref=part,
+                dst_ref=part,
+                send_sem=a_send.at[stage, j],
+                recv_sem=a_recv.at[stage, j],
+                device_id={"rows": mate(1)},
+                device_id_type=MESH,
             )
-            copies[-1].start()
-        landing[0, 0] = box[0, member]
-        return copies
+            for j, part in enumerate((landing.at[0, pl.ds(1, quad - 1)], landing.at[1]))
+        ]
 
     inner = jnp.logical_and(group > 0, group < groups_n - 1)
 
@@ -672,7 +680,7 @@
         return pltpu.make_async_remote_copy(
             src_ref=zbox.at[p, partner(k)],
             dst_ref=ring.at[way, p, k],
-            send_sem=r_send.at[way, p],
+            send_sem=r_send.at[0],
             recv_sem=r_recv.at[way, p],
             device_id={"rows": g * quad + partner(k), "feat": feats[p]},
             device_id_type=MESH,
@@ -682,7 +690,7 @@
         return pltpu.make_async_remote_copy(
             src_ref=ring.at[slot, p],
             dst_ref=ring.at[slot, p],
-            send_sem=r_send.at[slot, p],
+            send_sem=r_send.at[0],
             recv_sem=r_recv.at[slot, p],
             device_id={"rows": right},
             device_id_type=MESH,
@@ -692,7 +700,7 @@
         return pltpu.make_async_remote_copy(
             src_ref=ring.at[way, p],
             dst_ref=ring.at[2, p],
-            send_sem=r_send.at[2 + way, p],
+            send_sem=r_send.at[1],
             recv_sem=r_recv.at[2, p],
             device_id={"rows": left if way else right},
             device_id_type=MESH,
@@ -731,13 +739,16 @@
         pl.semaphore_wait(gate.at[1], 1)
 
     near = jnp.where(group == groups_n - 1, 1, 0)
+    for k in range(2):
+        to_group(near, 0, k).start()
+    for j, f, x in sides(after_own.T):
+        abox[j, f] = pack(x.astype(BF))
+    moved = [to_mates(abox, a_in, 0)]
     for way in (near, 1 - near):
         for p in range(2):
             for k in range(quad):
-                to_group(way, p, k).start()
-    for j, f, x in sides(after_own.T):
-        abox[j, f] = pack(x.astype(BF))
-    moved = [to_mates(abox, a_in, 0)]
+                if way is not near or p or k > 1:
+                    to_group(way, p, k).start()
     swaps[1].wait()
     fill(o_test[...], 1, t_cells, t_x)
     after_own, _ = feature_attention(t_cells, t_x)
@@ -746,13 +757,15 @@
     moved.append(to_mates(t_box, t_in, 1))
 
     loads[3].wait()
-    for i in (0, 2, 3):
+    for i in (2, 3):
         rw_t[i] = rw[i].astype(F32).T.astype(BF)
+    lane_head = lax.broadcasted_iota(jnp.int32, (1, width), 1) // HD
+    for h in range(heads):
+        one = jnp.where(lane_head == h, rw[1], jnp.zeros_like(rw[1]))
+        asks[h * width : (h + 1) * width] = (dot_t(one, rw[0]) * scale).astype(BF)
     loads[4].wait()
     up_t[...] = up[...].astype(F32).T.astype(BF)
     vals[...] = jnp.ones_like(vals)
-    early_q[...] = jnp.zeros_like(early_q)
-    late_q[...] = jnp.zeros_like(late_q)
 
     def arrive(stage):
         for c in moved[stage]:
@@ -762,7 +775,7 @@
             [unpack(landing[j, k]) for k in range(quad) for j in range(2)], axis=0
         ).astype(F32)
         normed = layer_norm(x).astype(BF)
-        return x, normed, (dot_t(rw_t[0], normed) * scale).astype(BF)
+        return x, normed, dot_t(asks[...], normed).astype(BF)
 
     n_mid = 2 * n_train
     n_late = 2 * n_train
@@ -771,14 +784,13 @@
     def place_queries(q, into, size, at):
         n = q.shape[1]
         for h in range(heads):
-            rows = slice(h * HD, (h + 1) * HD)
-            into[rows, h * size + at : h * size + at + n] = q[rows]
+            into[:, h * size + at : h * size + at + n] = q[h * width : (h + 1) * width]
 
     late = (late_q, late_s, late_e, late_sum, late_top, n_late)
     early = (early_q, early_s, early_e, early_sum, early_top, n_early)
 
     def key_value_rows(x, i):
-        keys[i] = dot(x, rw[1]).astype(BF)
+        keys[i] = x
         value = dot_t(rw_t[2], x).astype(BF)
         for h in range(heads):
             vals[i, h * lines : h * lines + HD] = value[h * HD : (h + 1) * HD]
@@ -821,62 +833,60 @@
         hidden[:, :n] = gelu(raised[:, :n]).astype(BF)
         return (after_row + dot(down[...], hidden[:, :n])).T.astype(BF)
 
+    at_start = group == 0
+    order = (jnp.where(at_start, 1, 0), jnp.where(at_start, 0, 1), 2)
+
+    def landed(i):
+        slot = order[i]
+
+        @pl.when(jnp.logical_not(jnp.logical_and(inner, slot < 2)))
+        def _():
+            for p in range(2):
+                whole(slot, p).wait_recv()
+
+    def fetch(i):
+        slot = order[i]
+        x = jnp.concatenate([unpack_blocks(ring[slot, p]) for p in range(2)], axis=0)
+        key_value_rows(x, (i + 1) % 2)
+
     relay(0)
-    relay(1)
     x, normed, q = arrive(0)
     place_queries(q[:, n_mid:], early_q, n_early, 0)
     place_queries(q[:, :n_late], late_q, n_late, 0)
     early_x[:, :n_mid] = x[n_late:].T
     late_x[...] = x[:n_late].T
     key_value_rows(normed, 0)
+    relay(1)
     attend([late], 0, True)
+    landed(0)
     x, _, q = arrive(1)
     place_queries(q, early_q, n_early, n_mid)
     early_x[:, n_mid:] = x.T
+    fetch(0)
+    attend([late], 1)
     attend([early], 0, True)
-
-    at_start, at_end = group == 0, group == groups_n - 1
-    order = (
-        jnp.where(at_start, 1, 0),
-        jnp.where(at_start, 2, jnp.where(at_end, 2, 1)),
-        jnp.where(at_start, 0, jnp.where(at_end, 1, 2)),
-    )
-
-    def fetch(i):
-        slot = order[i]
-
-        @pl.when(jnp.logical_not(jnp.logical_and(inner, slot < 2)))
-        def _():
-            for p in range(2):
-                whole(slot, p).wait_recv()
-
-        x = jnp.concatenate([unpack_blocks(ring[slot, p]) for p in range(2)], axis=0)
-        key_value_rows(x, (i + 1) % 2)
-
-    for i in range(2):
-        fetch(i)
-        attend([late, early], (i + 1) % 2)
+    attend([early], 1)
+    landed(1)
+    fetch(1)
+    attend([late, early], 0)
+    landed(2)
     fetch(2)
     loads[5].wait()
 
-    returns = []
-
     def give_back(k, done, tests):
         block = jnp.concatenate([done, tests[k * n_test : (k + 1) * n_test]], axis=0)
+        if k == 0:
+            back_in[member] = pack(block)
+            return
         back_out[k] = pack(block)
-        if k == 0:
-            c = pltpu.make_async_copy(back_out.at[0], back_in.at[member], b_send.at[0])
-        else:
-            c = pltpu.make_async_remote_copy(
-                src_ref=back_out.at[k],
-                dst_ref=back_in.at[member],
-                send_sem=b_send.at[k],
-                recv_sem=b_recv.at[k],
-                device_id={"rows": mate(k)},
-                device_id_type=MESH,
-            )
-        c.start()
-        returns.append(c)
+        pltpu.make_async_remote_copy(
+            src_ref=back_out.at[k],
+            dst_ref=back_in.at[member],
+            send_sem=b_send.at[0],
+            recv_sem=b_recv.at[0],
+            device_id={"rows": mate(k)},
+            device_id_type=MESH,
+        ).start()
 
     attend([early], 1)
     done = finish(early, early_x[...])
@@ -887,19 +897,32 @@
     done = finish(late, late_x[...])
     for k in (1, 0):
         give_back(k, done[k * n_train : (k + 1) * n_train], tests)
-    for c in returns:
-        c.wait()
+    pltpu.make_async_remote_copy(
+        src_ref=back_out.at[pl.ds(1, quad - 1)],
+        dst_ref=back_in.at[pl.ds(1, quad - 1)],
+        send_sem=b_send.at[0],
+        recv_sem=b_recv.at[0],
+        device_id={"rows": mate(1)},
+        device_id_type=MESH,
+    ).wait()
     for c in [*moved[0], *moved[1]]:
         c.wait_send()
-    for way in range(2):
-        for p in range(2):
-            whole(way, p).wait_send()
+
+    def sent(i):
+        pltpu.make_async_remote_copy(
+            src_ref=ring.at[pl.ds(0, 2)],
+            dst_ref=ring.at[pl.ds(0, 2)],
+            send_sem=r_send.at[i],
+            recv_sem=r_recv.at[0, 0],
+            device_id={"rows": right},
+            device_id_type=MESH,
+        ).wait_send()
+
+    sent(0)
 
     @pl.when(inner)
     def _():
-        for way in range(2):
-            for p in range(2):
-                onward(way, p).wait_send()
+        sent(1)
 
 
 def place_halves(back_ref, train_out, test_out):
@@ -970,6 +993,7 @@
                 vmem((both * n_half, heads * pair), BF),
                 vmem((width, both * n_half), BF),
                 vmem(rw.shape, BF),
+                vmem((heads * width, width), BF),
                 vmem(up.shape[::-1], BF),
                 vmem((span, heads * early), F32),
                 vmem((span, heads * late), F32),
@@ -995,12 +1019,12 @@
             flags = [
                 dma((2,)),
                 dma((2,)),
-                dma((2, 2, quad)),
-                dma((2, 2, quad)),
-                dma((4, 2)),
+                dma((2, 2)),
+                dma((2, 2)),
+                dma((2,)),
                 dma((3, 2)),
-                dma((quad,)),
-                dma((quad,)),
+                dma((1,)),
+                dma((1,)),
                 pltpu.SemaphoreType.REGULAR((2,)),
             ]
         else:

time: 26.4 us -> 25.4 us (0.962)
  Pallas kernels: 25.6 us -> 24.6 us
    pallas_call x1, Pallas kernels: 24.8 us -> 23.8 us  [body(): pl.pallas_call(functools.partial(body_fn, rows_n, feats_n), out_shape=plt...]
where the time goes in v3:
time: 25.4 us; the launch traced here: 25.2 us
  Pallas kernels  24.6 us (97%)
  between operations  0.64 us (3%)
    pallas_call x1, Pallas kernels, body(): pl.pallas_call(functools.partial(body_fn, rows_n, feats_n), out_shape=plt...  23.8 us
    pallas_call x1, Pallas kernels, body(): pl.pallas_call(place_fn, out_shape=(jax.ShapeDtypeStruct(train.shape, BF)...  0.79 us

profile of v3, /device:TPU:0, one launch (start us, length us, event | category | flops | bytes accessed | tf_op | source)
XLA Modules:
  0.0 25.2 jit_solution(10705239360108781400)
XLA Ops:
  0.6 23.8 %layer.1.back_ref = bf16[4,144,128]{2,1,0:T(8,128)(2,1)S(1)} custom-call(bf16[64,768]{1,0:T(8,128)(2,1)} %train_hbm.1, bf16[32,768]{1,0:T(8,128)(2,1)} %test_hbm.1, bf16[4,192,192]{2,1,0:T(8,128)(2,1)} %fw_hbm.1, bf16[4,192,192]{2,1,0:T(8,128)(2,1)} %rw_hbm.1, bf16[192,768]{1,0:T(8,128)(2,1)} %up_hbm.1, bf16[192,768]{1,0:T(8,128)(2,1)} %bitcast.1), custom_call_target="tpu_custom_call" | custom-call | tf_op jit(solution)/shard_map/layer/pallas_call | solution.py:1055
  24.4 0.8 %place.1 = (bf16[64,768]{1,0:T(8,128)(2,1)}, bf16[32,768]{1,0:T(8,128)(2,1)}) custom-call(bf16[4,144,128]{2,1,0:T(8,128)(2,1)S(1)} %layer.1.back_ref), custom_call_target="tpu_custom_call" | custom-call | tf_op jit(solution)/shard_map/place/pallas_call | solution.py:1076

commit v4 on v3

--- a/solution.py
+++ b/solution.py
@@ -575,13 +575,14 @@
         )
         for i, (s, d) in enumerate(
             [
-                (train_hbm.at[pl.ds(pl.multiple_of(other * n_half, n_half), n_half)], o_train),
-                (test_hbm.at[pl.ds(pl.multiple_of(other * n_quart, n_quart), n_quart)], o_test),
+                (train_ref.at[pl.ds(pl.multiple_of(other * n_half, n_half), n_half)], o_train),
+                (test_ref.at[pl.ds(pl.multiple_of(other * n_quart, n_quart), n_quart)], o_test),
             ]
         )
     ]
-    for c in swaps:
-        c.start()
+    for i in range(2):
+        loads[2 * i].wait()
+        swaps[i].start()
 
     tile = 16
     cell = quad * tile
@@ -713,12 +714,10 @@
                 whole(way, p).wait_recv()
                 onward(way, p).start()
 
-    loads[0].wait()
     loads[1].wait()
     fill(train_ref[pl.ds(pl.multiple_of(my_feat * n_half, n_half), n_half)], 0, f_cells, f_x)
     for i in (0, 2, 3):
         fw_t[i] = fw[i].astype(F32).T.astype(BF)
-    loads[2].wait()
     fill(test_ref[pl.ds(pl.multiple_of(my_feat * n_quart, n_quart), n_quart)], 0, t_cells, t_x)
     fq[...] = jnp.zeros_like(fq)
     fv[...] = jnp.ones_like(fv)
@@ -739,6 +738,20 @@
         pl.semaphore_wait(gate.at[1], 1)
 
     near = jnp.where(group == groups_n - 1, 1, 0)
+    at_end = group == groups_n - 1
+
+    @pl.when(at_end)
+    def _():
+        for k in range(quad):
+            pltpu.make_async_remote_copy(
+                src_ref=zbox.at[my_feat, partner(k)],
+                dst_ref=ring.at[0, my_feat, k],
+                send_sem=r_send.at[0],
+                recv_sem=r_recv.at[0, my_feat],
+                device_id={"rows": right_group * quad + partner(k), "feat": 0},
+                device_id_type=MESH,
+            ).start()
+
     for k in range(2):
         to_group(near, 0, k).start()
     for j, f, x in sides(after_own.T):
@@ -747,7 +760,13 @@
     for way in (near, 1 - near):
         for p in range(2):
             for k in range(quad):
-                if way is not near or p or k > 1:
+                if way is near:
+                    if p or k > 1:
+                        to_group(way, p, k).start()
+                    continue
+
+                @pl.when(jnp.logical_not(jnp.logical_and(at_end, my_feat == p)))
+                def _():
                     to_group(way, p, k).start()
     swaps[1].wait()
     fill(o_test[...], 1, t_cells, t_x)
@@ -767,15 +786,8 @@
     up_t[...] = up[...].astype(F32).T.astype(BF)
     vals[...] = jnp.ones_like(vals)
 
-    def arrive(stage):
-        for c in moved[stage]:
-            c.wait_recv()
-        landing = (a_in, t_in)[stage]
-        x = jnp.concatenate(
-            [unpack(landing[j, k]) for k in range(quad) for j in range(2)], axis=0
-        ).astype(F32)
-        normed = layer_norm(x).astype(BF)
-        return x, normed, dot_t(asks[...], normed).astype(BF)
+    def arrived(landing):
+        return [unpack(landing[j, k]) for k in range(quad) for j in range(2)]
 
     n_mid = 2 * n_train
     n_late = 2 * n_train
@@ -795,26 +807,34 @@
         for h in range(heads):
             vals[i, h * lines : h * lines + HD] = value[h * HD : (h + 1) * HD]
 
-    def attend(asked, i, first=False):
+    span = quad * n_train
+
+    def attend(asked, slots, first=False):
         per_head = [
             (part, h, slice(h * part[5], (h + 1) * part[5]), slice(h * lines, (h + 1) * lines))
             for part in asked
             for h in range(heads)
         ]
-        key = keys[i]
-        for (q, s, _, _, _, _), h, c, _ in per_head:
-            s[:, c] = dot(key, q[:, c])
+        spans = [slice(n * span, (n + 1) * span) for n in range(len(slots))]
+        for at, i in zip(spans, slots):
+            key = keys[i]
+            for (q, s, _, _, _, _), h, c, _ in per_head:
+                s[at, c] = dot(key, q[:, c])
+        whole_span = slice(0, len(slots) * span)
         for (_, s, e, total, tops, _), h, c, r in per_head:
-            top = jnp.max(s[:, c], axis=0, keepdims=True)
+            top = jnp.max(s[whole_span, c], axis=0, keepdims=True)
             if not first:
                 old = tops[0:1, c]
                 top = jnp.maximum(top, old)
                 total[r] = total[r] * jnp.exp2(old - top)
-            e[:, c] = jnp.exp2(s[:, c] - top).astype(BF)
+            e[whole_span, c] = jnp.exp2(s[whole_span, c] - top).astype(BF)
             tops[0:1, c] = top
         for (_, _, e, total, _, _), h, c, r in per_head:
-            out = dot(vals[i, r], e[:, c])
-            total[r] = out if first else total[r] + out
+            out = None if first else total[r]
+            for at, i in zip(spans, slots):
+                part = dot(vals[i, r], e[at, c])
+                out = part if out is None else out + part
+            total[r] = out
 
     def finish(part, before):
         total = part[3]
@@ -850,25 +870,24 @@
         key_value_rows(x, (i + 1) % 2)
 
     relay(0)
-    x, normed, q = arrive(0)
-    place_queries(q[:, n_mid:], early_q, n_early, 0)
-    place_queries(q[:, :n_late], late_q, n_late, 0)
-    early_x[:, :n_mid] = x[n_late:].T
+    for c in moved[0]:
+        c.wait_recv()
+    relay(1)
+    for c in moved[1]:
+        c.wait_recv()
+    landed(0)
+    x = jnp.concatenate(arrived(a_in) + arrived(t_in), axis=0).astype(F32)
+    early_x[...] = x[n_late:].T
     late_x[...] = x[:n_late].T
-    key_value_rows(normed, 0)
-    relay(1)
-    attend([late], 0, True)
-    landed(0)
-    x, _, q = arrive(1)
-    place_queries(q, early_q, n_early, n_mid)
-    early_x[:, n_mid:] = x.T
+    for part, into, n in ((early_x, early_q, n_early), (late_x, late_q, n_late)):
+        columns = normed_columns(part[...]).astype(BF)
+        place_queries(dot(asks[...], columns).astype(BF), into, n, 0)
+    key_value_rows(layer_norm(x[: quad * n_train]).astype(BF), 0)
     fetch(0)
-    attend([late], 1)
-    attend([early], 0, True)
-    attend([early], 1)
+    attend([late, early], (0, 1), True)
     landed(1)
     fetch(1)
-    attend([late, early], 0)
+    attend([late, early], (0,))
     landed(2)
     fetch(2)
     loads[5].wait()
@@ -888,23 +907,24 @@
             device_id_type=MESH,
         ).start()
 
-    attend([early], 1)
+    attend([early], (1,))
     done = finish(early, early_x[...])
     tests = done[n_mid:]
     for k in (2, 3):
         give_back(k, done[(k - 2) * n_train : (k - 1) * n_train], tests)
-    attend([late], 1)
+    attend([late], (1,))
     done = finish(late, late_x[...])
     for k in (1, 0):
         give_back(k, done[k * n_train : (k + 1) * n_train], tests)
-    pltpu.make_async_remote_copy(
+    returned = pltpu.make_async_remote_copy(
         src_ref=back_out.at[pl.ds(1, quad - 1)],
         dst_ref=back_in.at[pl.ds(1, quad - 1)],
         send_sem=b_send.at[0],
         recv_sem=b_recv.at[0],
         device_id={"rows": mate(1)},
         device_id_type=MESH,
-    ).wait()
+    )
+    returned.wait()
     for c in [*moved[0], *moved[1]]:
         c.wait_send()
 
@@ -995,10 +1015,10 @@
                 vmem(rw.shape, BF),
                 vmem((heads * width, width), BF),
                 vmem(up.shape[::-1], BF),
-                vmem((span, heads * early), F32),
-                vmem((span, heads * late), F32),
-                vmem((span, heads * early), BF),
-                vmem((span, heads * late), BF),
+                vmem((2 * span, heads * early), F32),
+                vmem((2 * span, heads * late), F32),
+                vmem((2 * span, heads * early), BF),
+                vmem((2 * span, heads * late), BF),
                 vmem((heads * (HD + 16), early), F32),
                 vmem((heads * (HD + 16), late), F32),
                 vmem((8, heads * early), F32),

time: 25.4 us -> 24.8 us (0.976)
  Pallas kernels: 24.6 us -> 24 us
    pallas_call x1, Pallas kernels: 23.8 us -> 23.2 us  [body(): pl.pallas_call(functools.partial(body_fn, rows_n, feats_n), out_shape=plt...]
where the time goes in v4:
time: 24.8 us; the launch traced here: 24.7 us
  Pallas kernels  24 us (97%)
  between operations  0.64 us (3%)
    pallas_call x1, Pallas kernels, body(): pl.pallas_call(functools.partial(body_fn, rows_n, feats_n), out_shape=plt...  23.2 us
    pallas_call x1, Pallas kernels, body(): pl.pallas_call(place_fn, out_shape=(jax.ShapeDtypeStruct(train.shape, BF)...  0.79 us

profile of v4, /device:TPU:0, one launch (start us, length us, event | category | flops | bytes accessed | tf_op | source)
XLA Modules:
  0.0 24.7 jit_solution(991498286432322172)
XLA Ops:
  0.6 23.2 %layer.1.back_ref = bf16[4,144,128]{2,1,0:T(8,128)(2,1)S(1)} custom-call(bf16[64,768]{1,0:T(8,128)(2,1)} %train_hbm.1, bf16[32,768]{1,0:T(8,128)(2,1)} %test_hbm.1, bf16[4,192,192]{2,1,0:T(8,128)(2,1)} %fw_hbm.1, bf16[4,192,192]{2,1,0:T(8,128)(2,1)} %rw_hbm.1, bf16[192,768]{1,0:T(8,128)(2,1)} %up_hbm.1, bf16[192,768]{1,0:T(8,128)(2,1)} %bitcast.1), custom_call_target="tpu_custom_call" | custom-call | tf_op jit(solution)/shard_map/layer/pallas_call | solution.py:1075
  23.9 0.8 %place.1 = (bf16[64,768]{1,0:T(8,128)(2,1)}, bf16[32,768]{1,0:T(8,128)(2,1)}) custom-call(bf16[4,144,128]{2,1,0:T(8,128)(2,1)S(1)} %layer.1.back_ref), custom_call_target="tpu_custom_call" | custom-call | tf_op jit(solution)/shard_map/place/pallas_call | solution.py:1096

commit v5 on v4

--- a/solution.py
+++ b/solution.py
@@ -606,7 +606,7 @@
         normed = layer_norm(cells).astype(BF)
         for b in range(n):
             to = slice((2 * b + side) * cell, (2 * b + side + 1) * cell)
-            cells_ref[to] = cells[b * cell : (b + 1) * cell]
+            cells_ref[to] = cells[b * cell : (b + 1) * cell].astype(BF)
             x_ref[to] = normed[b * cell : (b + 1) * cell]
 
     def normed_columns(x):
@@ -638,7 +638,7 @@
                 )
                 part = out[:HD] * (1.0 / out[HD : HD + 1])
                 fm[h * HD : (h + 1) * HD, at] = part.astype(BF)
-        after = cells_ref[...].T + dot(fw_t[3], fm[:, :n])
+        after = cells_ref[...].T.astype(F32) + dot(fw_t[3], fm[:, :n])
         return after, normed_columns(after)
 
     def sides(x):
@@ -710,7 +710,7 @@
     def relay(p):
         @pl.when(inner)
         def _():
-            for way in range(2):
+            for way in (1, 0):
                 whole(way, p).wait_recv()
                 onward(way, p).start()
 
@@ -730,14 +730,14 @@
     swaps[0].wait()
     fill(o_train[...], 1, f_cells, f_x)
     after_own, normed_own = feature_attention(f_cells, f_x)
-    for j, f, x in sides(normed_own.T):
-        zbox[j, f] = pack(x.astype(BF))
+    for j, f, x in sides(normed_own.astype(BF).T):
+        zbox[j, f] = pack(x)
 
     @pl.when(even)
     def _():
         pl.semaphore_wait(gate.at[1], 1)
 
-    near = jnp.where(group == groups_n - 1, 1, 0)
+    near = jnp.where(group >= 1, 1, 0)
     at_end = group == groups_n - 1
 
     @pl.when(at_end)
@@ -754,8 +754,8 @@
 
     for k in range(2):
         to_group(near, 0, k).start()
-    for j, f, x in sides(after_own.T):
-        abox[j, f] = pack(x.astype(BF))
+    for j, f, x in sides(after_own.astype(BF).T):
+        abox[j, f] = pack(x)
     moved = [to_mates(abox, a_in, 0)]
     for way in (near, 1 - near):
         for p in range(2):
@@ -771,8 +771,8 @@
     swaps[1].wait()
     fill(o_test[...], 1, t_cells, t_x)
     after_own, _ = feature_attention(t_cells, t_x)
-    for j, f, x in sides(after_own.T):
-        t_box[j, f] = pack(x.astype(BF))
+    for j, f, x in sides(after_own.astype(BF).T):
+        t_box[j, f] = pack(x)
     moved.append(to_mates(t_box, t_in, 1))
 
     loads[3].wait()
@@ -849,9 +849,12 @@
         after_row = before + dot(rw_t[3], mix)
         normed = normed_columns(after_row).astype(BF)
         n = normed.shape[1]
-        raised[:, :n] = dot(up_t[...], normed)
-        hidden[:, :n] = gelu(raised[:, :n]).astype(BF)
-        return (after_row + dot(down[...], hidden[:, :n])).T.astype(BF)
+        step = width
+        for i in range(up_t.shape[0] // step):
+            at = slice(i * step, (i + 1) * step)
+            raised[at, :n] = dot(up_t[at], normed)
+            hidden[at, :n] = gelu(raised[at, :n]).astype(BF)
+        return (after_row + dot(down[...], hidden[:, :n])).astype(BF).T
 
     at_start = group == 0
     order = (jnp.where(at_start, 1, 0), jnp.where(at_start, 0, 1), 2)
@@ -870,19 +873,17 @@
         key_value_rows(x, (i + 1) % 2)
 
     relay(0)
-    for c in moved[0]:
-        c.wait_recv()
     relay(1)
-    for c in moved[1]:
+    for c in [*moved[0], *moved[1]]:
         c.wait_recv()
     landed(0)
-    x = jnp.concatenate(arrived(a_in) + arrived(t_in), axis=0).astype(F32)
-    early_x[...] = x[n_late:].T
-    late_x[...] = x[:n_late].T
+    x = jnp.concatenate(arrived(a_in) + arrived(t_in), axis=0)
+    early_x[...] = x[n_late:].T.astype(F32)
+    late_x[...] = x[:n_late].T.astype(F32)
     for part, into, n in ((early_x, early_q, n_early), (late_x, late_q, n_late)):
         columns = normed_columns(part[...]).astype(BF)
         place_queries(dot(asks[...], columns).astype(BF), into, n, 0)
-    key_value_rows(layer_norm(x[: quad * n_train]).astype(BF), 0)
+    key_value_rows(layer_norm(x[: quad * n_train].astype(F32)).astype(BF), 0)
     fetch(0)
     attend([late, early], (0, 1), True)
     landed(1)
@@ -948,13 +949,13 @@
 def place_halves(back_ref, train_out, test_out):
     quad = back_ref.shape[0]
     result = jnp.concatenate([unpack(back_ref[f]) for f in range(quad)], axis=1)
-    in_order = lax.axis_index("feat") == 0
+    mine = lax.axis_index("feat")
     begin = 0
     for out in (train_out, test_out):
         half = out.shape[0] // 2
-        one, two = (result[begin + j * half : begin + (j + 1) * half] for j in range(2))
-        out[:half] = jnp.where(in_order, one, two)
-        out[half:] = jnp.where(in_order, two, one)
+        for j, place_of in enumerate((mine, 1 - mine)):
+            to = pl.ds(pl.multiple_of(place_of * half, half), half)
+            out[to] = result[begin + j * half : begin + (j + 1) * half]
         begin += 2 * half
 
 
@@ -1002,9 +1003,9 @@
                 vmem((width, early), F32),
                 vmem((width, late), F32),
                 vmem(fw.shape, BF),
-                vmem((both * n_half, width), F32),
                 vmem((both * n_half, width), BF),
-                vmem((both * n_quart, width), F32),
+                vmem((both * n_half, width), BF),
+                vmem((both * n_quart, width), BF),
                 vmem((both * n_quart, width), BF),
                 vmem((width, heads * both * n_half), BF),
                 vmem((both * n_half, width), BF),

time: 24.8 us -> 24.5 us (0.988)
  Pallas kernels: 24 us -> 23.7 us
    pallas_call x1, Pallas kernels: 23.2 us -> 22.9 us  [body(): pl.pallas_call(functools.partial(body_fn, rows_n, feats_n), out_shape=plt...]
where the time goes in v5:
time: 24.5 us; the launch traced here: 24.4 us
  Pallas kernels  23.7 us (97%)
  between operations  0.64 us (3%)
    pallas_call x1, Pallas kernels, body(): pl.pallas_call(functools.partial(body_fn, rows_n, feats_n), out_shape=plt...  22.9 us
    pallas_call x1, Pallas kernels, body(): pl.pallas_call(place_fn, out_shape=(jax.ShapeDtypeStruct(train.shape, BF)...  0.8 us

profile of v5, /device:TPU:0, one launch (start us, length us, event | category | flops | bytes accessed | tf_op | source)
XLA Modules:
  0.0 24.4 jit_solution(16318796155686321775)
XLA Ops:
  0.6 22.9 %layer.1.back_ref = bf16[4,144,128]{2,1,0:T(8,128)(2,1)S(1)} custom-call(bf16[64,768]{1,0:T(8,128)(2,1)} %train_hbm.1, bf16[32,768]{1,0:T(8,128)(2,1)} %test_hbm.1, bf16[4,192,192]{2,1,0:T(8,128)(2,1)} %fw_hbm.1, bf16[4,192,192]{2,1,0:T(8,128)(2,1)} %rw_hbm.1, bf16[192,768]{1,0:T(8,128)(2,1)} %up_hbm.1, bf16[192,768]{1,0:T(8,128)(2,1)} %bitcast.1), custom_call_target="tpu_custom_call" | custom-call | tf_op jit(solution)/shard_map/layer/pallas_call | solution.py:1076
  23.6 0.8 %place.1 = (bf16[64,768]{1,0:T(8,128)(2,1)}, bf16[32,768]{1,0:T(8,128)(2,1)}) custom-call(bf16[4,144,128]{2,1,0:T(8,128)(2,1)S(1)} %layer.1.back_ref), custom_call_target="tpu_custom_call" | custom-call | tf_op jit(solution)/shard_map/place/pallas_call | solution.py:1097

commit v6 on v5

--- a/solution.py
+++ b/solution.py
@@ -801,11 +801,12 @@
     late = (late_q, late_s, late_e, late_sum, late_top, n_late)
     early = (early_q, early_s, early_e, early_sum, early_top, n_early)
 
-    def key_value_rows(x, i):
-        keys[i] = x
+    def key_value_rows(x, i, begin=0):
+        to = slice(begin, begin + x.shape[0])
+        keys[i, to] = x
         value = dot_t(rw_t[2], x).astype(BF)
         for h in range(heads):
-            vals[i, h * lines : h * lines + HD] = value[h * HD : (h + 1) * HD]
+            vals[i, h * lines : h * lines + HD, to] = value[h * HD : (h + 1) * HD]
 
     span = quad * n_train
 
@@ -815,12 +816,15 @@
             for part in asked
             for h in range(heads)
         ]
-        spans = [slice(n * span, (n + 1) * span) for n in range(len(slots))]
-        for at, i in zip(spans, slots):
-            key = keys[i]
+        spans = []
+        for _, own in slots:
+            begin = spans[-1].stop if spans else 0
+            spans.append(slice(begin, begin + own.stop - own.start))
+        for at, (i, own) in zip(spans, slots):
+            key = keys[i, own]
             for (q, s, _, _, _, _), h, c, _ in per_head:
                 s[at, c] = dot(key, q[:, c])
-        whole_span = slice(0, len(slots) * span)
+        whole_span = slice(0, spans[-1].stop)
         for (_, s, e, total, tops, _), h, c, r in per_head:
             top = jnp.max(s[whole_span, c], axis=0, keepdims=True)
             if not first:
@@ -831,8 +835,8 @@
             tops[0:1, c] = top
         for (_, _, e, total, _, _), h, c, r in per_head:
             out = None if first else total[r]
-            for at, i in zip(spans, slots):
-                part = dot(vals[i, r], e[at, c])
+            for at, (i, own) in zip(spans, slots):
+                part = dot(vals[i, r, own], e[at, c])
                 out = part if out is None else out + part
             total[r] = out
 
@@ -885,12 +889,26 @@
         place_queries(dot(asks[...], columns).astype(BF), into, n, 0)
     key_value_rows(layer_norm(x[: quad * n_train].astype(F32)).astype(BF), 0)
     fetch(0)
-    attend([late, early], (0, 1), True)
+    every = slice(0, span)
+    attend([late, early], ((0, every), (1, every)), True)
     landed(1)
     fetch(1)
-    attend([late, early], (0,))
-    landed(2)
-    fetch(2)
+    attend([late, early], ((0, every),))
+    halves = [(1, slice(p * span // 2, (p + 1) * span // 2)) for p in range(2)]
+
+    @pl.when(at_start)
+    def _():
+        for p, half in enumerate(halves):
+            whole(2, p).wait_recv()
+            key_value_rows(unpack_blocks(ring[2, p]), 1, half[1].start)
+            attend([early] if p else [late, early], (half,))
+
+    @pl.when(jnp.logical_not(at_start))
+    def _():
+        landed(2)
+        fetch(2)
+        attend([early], ((1, every),))
+
     loads[5].wait()
 
     def give_back(k, done, tests):
@@ -908,12 +926,19 @@
             device_id_type=MESH,
         ).start()
 
-    attend([early], (1,))
     done = finish(early, early_x[...])
     tests = done[n_mid:]
     for k in (2, 3):
         give_back(k, done[(k - 2) * n_train : (k - 1) * n_train], tests)
-    attend([late], (1,))
+
+    @pl.when(at_start)
+    def _():
+        attend([late], (halves[1],))
+
+    @pl.when(jnp.logical_not(at_start))
+    def _():
+        attend([late], ((1, every),))
+
     done = finish(late, late_x[...])
     for k in (1, 0):
         give_back(k, done[k * n_train : (k + 1) * n_train], tests)

time: 24.5 us -> 24.3 us (level)
  no operation moved by 1% of the time
where the time goes in v6:
time: 24.3 us; the launch traced here: 24.2 us
  Pallas kernels  23.5 us (97%)
  between operations  0.64 us (3%)
    pallas_call x1, Pallas kernels, body(): pl.pallas_call(functools.partial(body_fn, rows_n, feats_n), out_shape=plt...  22.7 us
    pallas_call x1, Pallas kernels, body(): pl.pallas_call(place_fn, out_shape=(jax.ShapeDtypeStruct(train.shape, BF)...  0.8 us

profile of v6, /device:TPU:0, one launch (start us, length us, event | category | flops | bytes accessed | tf_op | source)
XLA Modules:
  0.0 24.2 jit_solution(1449059674084595977)
XLA Ops:
  0.6 22.7 %layer.1.back_ref = bf16[4,144,128]{2,1,0:T(8,128)(2,1)S(1)} custom-call(bf16[64,768]{1,0:T(8,128)(2,1)} %train_hbm.1, bf16[32,768]{1,0:T(8,128)(2,1)} %test_hbm.1, bf16[4,192,192]{2,1,0:T(8,128)(2,1)} %fw_hbm.1, bf16[4,192,192]{2,1,0:T(8,128)(2,1)} %rw_hbm.1, bf16[192,768]{1,0:T(8,128)(2,1)} %up_hbm.1, bf16[192,768]{1,0:T(8,128)(2,1)} %bitcast.1), custom_call_target="tpu_custom_call" | custom-call | tf_op jit(solution)/shard_map/layer/pallas_call | solution.py:1101
  23.4 0.8 %place.1 = (bf16[64,768]{1,0:T(8,128)(2,1)}, bf16[32,768]{1,0:T(8,128)(2,1)}) custom-call(bf16[4,144,128]{2,1,0:T(8,128)(2,1)S(1)} %layer.1.back_ref), custom_call_target="tpu_custom_call" | custom-call | tf_op jit(solution)/shard_map/place/pallas_call | solution.py:1122

commit v7 on v6

--- a/solution.py
+++ b/solution.py
@@ -580,9 +580,8 @@
             ]
         )
     ]
-    for i in range(2):
-        loads[2 * i].wait()
-        swaps[i].start()
+    loads[0].wait()
+    swaps[0].start()
 
     tile = 16
     cell = quad * tile
@@ -718,6 +717,8 @@
     fill(train_ref[pl.ds(pl.multiple_of(my_feat * n_half, n_half), n_half)], 0, f_cells, f_x)
     for i in (0, 2, 3):
         fw_t[i] = fw[i].astype(F32).T.astype(BF)
+    loads[2].wait()
+    swaps[1].start()
     fill(test_ref[pl.ds(pl.multiple_of(my_feat * n_quart, n_quart), n_quart)], 0, t_cells, t_x)
     fq[...] = jnp.zeros_like(fq)
     fv[...] = jnp.ones_like(fv)

time: 24.3 us -> 24.3 us (level)
  no operation moved by 1% of the time
where the time goes in v7:
time: 24.3 us; the launch traced here: 24.2 us
  Pallas kernels  23.5 us (97%)
  between operations  0.64 us (3%)
    pallas_call x1, Pallas kernels, body(): pl.pallas_call(functools.partial(body_fn, rows_n, feats_n), out_shape=plt...  22.7 us
    pallas_call x1, Pallas kernels, body(): pl.pallas_call(place_fn, out_shape=(jax.ShapeDtypeStruct(train.shape, BF)...  0.8 us

profile of v7, /device:TPU:0, one launch (start us, length us, event | category | flops | bytes accessed | tf_op | source)
XLA Modules:
  0.0 24.2 jit_solution(5530145484044722292)
XLA Ops:
  0.6 22.7 %layer.1.back_ref = bf16[4,144,128]{2,1,0:T(8,128)(2,1)S(1)} custom-call(bf16[64,768]{1,0:T(8,128)(2,1)} %train_hbm.1, bf16[32,768]{1,0:T(8,128)(2,1)} %test_hbm.1, bf16[4,192,192]{2,1,0:T(8,128)(2,1)} %fw_hbm.1, bf16[4,192,192]{2,1,0:T(8,128)(2,1)} %rw_hbm.1, bf16[192,768]{1,0:T(8,128)(2,1)} %up_hbm.1, bf16[192,768]{1,0:T(8,128)(2,1)} %bitcast.1), custom_call_target="tpu_custom_call" | custom-call | tf_op jit(solution)/shard_map/layer/pallas_call | solution.py:1102
  23.4 0.8 %place.1 = (bf16[64,768]{1,0:T(8,128)(2,1)}, bf16[32,768]{1,0:T(8,128)(2,1)}) custom-call(bf16[4,144,128]{2,1,0:T(8,128)(2,1)S(1)} %layer.1.back_ref), custom_call_target="tpu_custom_call" | custom-call | tf_op jit(solution)/shard_map/place/pallas_call | solution.py:1123
